TPU v7x, 32 devices: a whole 2x2x4 slice. The times are simulated.
32 devices in a mesh: gy: 8 (over y, x, core), gx: 4 (over z).
Axes of the slice: x: 2, y: 2, z: 4, core: 2. Of those that a mesh axis runs over, the one named last changes fastest.
Arguments:
- tracer: float32 [8, 1024, 1024], P(None, 'gy', 'gx'), may hold values from -6 to 6
- east_speed: float32 [8, 1024, 1024], P(None, 'gy', 'gx'), may hold values from -0.25 to 0.25
- north_speed: float32 [8, 1024, 1024], P(None, 'gy', 'gx'), may hold values from -0.25 to 0.25
- columns: int32 [1024, 1024], P('gy', 'gx'), may hold values from 0 to 8
- thickness: float32 [8], replicated, may hold values from 0.5 to 2
- surface_flux: float32 [1024, 1024], P('gy', 'gx'), may hold values from -6 to 6
- helm: float32 [1024, 1024], P('gy', 'gx'), may hold values from 0.2 to 4
Outputs:
- tracer_new: float32 [8, 1024, 1024], P(None, 'gy', 'gx')
- heights: float32 [1024, 1024], P('gy', 'gx')
Inputs may be any that keep to these rules, and one draw needn't show every extreme that they name: `columns`: ocean levels per column; 0 means land.
All inputs are finite; a program needn't handle non-finite values.
Results may differ from a plain program's by a relative error of at most 0.0001.
Values sent between devices are 32-bit elements; how exact they have to be, the bound alone decides.
A program may use at most 64 MiB of HBM per device.

v0:
```python
import functools

import jax
import jax.numpy as jnp
from jax import lax
from jax.experimental import pallas as pl
from jax.experimental.pallas import tpu as pltpu
from jax.sharding import PartitionSpec as P

TSTEPS = 2
ITERS = 3
MESH = pl.DeviceIdType.MESH
SUB = 8
LANE = 128
AROUND = ((1, 0), (-1, 0), (0, 1), (0, -1), (1, 1), (1, -1), (-1, 1), (-1, -1))


def roll(array, shift, axis):
    shift = shift % array.shape[axis]
    return pltpu.roll(array, shift, axis) if shift else array


def iota(shape, dim):
    return lax.broadcasted_iota(jnp.int32, shape, dim)


def kernel(
    ny,
    nx,
    tracer_ref,
    east_ref,
    north_ref,
    columns_ref,
    thick_hbm,
    surface_ref,
    helm_ref,
    tracer_out,
    heights_out,
    c_ext,
    e_ext,
    n_ext,
    col_in,
    surf_in,
    flat_ext,
    face_levels,
    pack,
    to_left,
    to_right,
    from_left,
    from_right,
    corner_recv,
    up_send,
    down_send,
    up_recv,
    down_recv,
    forcing,
    start_vec,
    flat_pack,
    edge_pack,
    row_recv,
    edge_recv,
    edge_corner_recv,
    part,
    slots,
    thickness_ref,
    in_sem,
    out_sem,
    send_sem,
    recv_sem,
    sum_send_sem,
    sum_recv_sem,
):
    levels, rows, cols = tracer_ref.shape
    ext_rows, ext_cols = rows + SUB, cols + LANE
    my_y, my_x = lax.axis_index("gy"), lax.axis_index("gx")
    count = ny * nx
    my_id = my_y * nx + my_x

    def place(offset):
        target = lax.rem(my_id + offset, count)
        return (target // nx, lax.rem(target, nx))

    def near(dy, dx):
        return (lax.rem(my_y + dy + ny, ny), lax.rem(my_x + dx + nx, nx))

    loads = [
        pltpu.make_async_copy(columns_ref, col_in, in_sem.at[0]),
        pltpu.make_async_copy(helm_ref, flat_ext.at[1, 0:rows, 0:cols], in_sem.at[1]),
        pltpu.make_async_copy(tracer_ref, c_ext.at[:, 0:rows, 0:cols], in_sem.at[2]),
        pltpu.make_async_copy(east_ref, e_ext.at[:, 0:rows, 0:cols], in_sem.at[3]),
        pltpu.make_async_copy(north_ref, n_ext.at[:, 0:rows, 0:cols], in_sem.at[4]),
        pltpu.make_async_copy(surface_ref, surf_in, in_sem.at[5]),
        pltpu.make_async_copy(thick_hbm, thickness_ref, in_sem.at[6]),
    ]
    for load in loads:
        load.start()
    barrier = pltpu.get_barrier_semaphore()
    for offset in range(1, count):
        pl.semaphore_signal(barrier, inc=1, device_id=place(offset), device_id_type=MESH)
    for load in loads:
        load.wait()

    fields = (c_ext, e_ext, n_ext)
    flat_ext[0, 0:rows, 0:cols] = col_in[...].astype(jnp.float32)

    lane_full = iota((rows, LANE), 1)
    lane_half = lane_full < LANE // 2
    group = lane_full // 4

    def both_edges(ref, index):
        return jnp.where(lane_half, ref[index, 0:rows, 0:LANE], ref[index, 0:rows, cols - LANE : cols])

    sources = [(fields[f], k, f) for k in range(levels) for f in range(3)]
    sources += [(flat_ext, 0, 3), (flat_ext, 1, 4)]
    packed = jnp.zeros((rows, LANE), jnp.float32)
    for slot, (ref, index, _) in enumerate(sources):
        packed = jnp.where(group == slot, roll(both_edges(ref, index), 4 * slot + 2, 1), packed)
    pack[...] = packed
    turned = packed.T
    sub_rows = iota((SUB, rows), 0) % 4 < 2
    for p in range(to_left.shape[0]):
        one, two = turned[2 * SUB * p :][:SUB], turned[2 * SUB * p + SUB :][:SUB]
        to_right[p] = jnp.where(sub_rows, one, roll(two, 2, 0))
        to_left[p] = jnp.where(sub_rows, roll(two, -2, 0), one)

    sub = iota((SUB, cols), 0)
    for k in range(levels):
        quads = [(ref, k) for ref in fields] + [(flat_ext, min(k, 1))]
        up = jnp.zeros((SUB, cols), jnp.float32)
        down = jnp.zeros((SUB, cols), jnp.float32)
        for f, (ref, index) in enumerate(quads):
            mine = sub // 2 == f
            up = jnp.where(mine, roll(ref[index, rows - SUB : rows, 0:cols], 2 * f + 2, 0), up)
            down = jnp.where(mine, roll(ref[index, 0:SUB, 0:cols], 2 * f, 0), down)
        up_send[k] = up
        down_send[k] = down

    pl.semaphore_wait(barrier, count - 1)

    first_rows, last_rows = pl.ds(0, SUB), pl.ds(rows - SUB, SUB)
    first = [
        (up_send, up_recv),
        (down_send, down_recv),
        (to_right, from_left),
        (to_left, from_right),
        (pack.at[last_rows], corner_recv.at[0]),
        (pack.at[last_rows], corner_recv.at[1]),
        (pack.at[first_rows], corner_recv.at[2]),
        (pack.at[first_rows], corner_recv.at[3]),
    ]

    def exchange(pairs, base):
        copies = []
        for which, (source, target) in enumerate(pairs):
            copies.append(
                pltpu.make_async_remote_copy(
                    src_ref=source,
                    dst_ref=target,
                    send_sem=send_sem.at[base + which],
                    recv_sem=recv_sem.at[base + which],
                    device_id=near(*AROUND[which]),
                    device_id_type=MESH,
                )
            )
        for copy in reversed(copies):
            copy.start()
        return copies

    copies = exchange(first, 0)
    for copy in copies:
        copy.wait_recv()

    pieces = []
    for p in range(to_left.shape[0]):
        x, y = from_left[p], from_right[p]
        pieces.append(jnp.where(sub_rows, x, y))
        pieces.append(jnp.where(sub_rows, roll(x, -2, 0), roll(y, 2, 0)))
    spare = LANE - 2 * SUB * to_left.shape[0]
    if spare:
        pieces.append(jnp.zeros((spare, rows), jnp.float32))
    sides = jnp.concatenate(pieces, axis=0).T
    small_right = (iota((SUB, LANE), 1) % 4) >= 2
    small_below = iota((SUB, LANE), 0) < SUB // 2
    south = jnp.where(small_right, corner_recv[1], corner_recv[0])
    north = jnp.where(small_right, corner_recv[3], corner_recv[2])
    corner = jnp.where(small_below, north, south)
    for slot, (ref, index, _) in enumerate(sources):
        ref[index, 0:rows, cols:ext_cols] = roll(sides, -4 * slot - 2, 1)
        ref[index, rows:ext_rows, cols:ext_cols] = roll(corner, -4 * slot - 2, 1)
    for k in range(levels):
        quads = [(ref, k) for ref in fields] + ([(flat_ext, k)] if k < 2 else [])
        for f, (ref, index) in enumerate(quads):
            ref[index, rows:ext_rows, 0:cols] = jnp.where(
                sub < SUB // 2,
                roll(down_recv[k], -2 * f, 0),
                roll(up_recv[k], -2 * f - 2, 0),
            )

    row_ids = iota((SUB, ext_cols), 0)
    beyond = (row_ids >= SUB // 2) & (my_y == 0) | (row_ids < SUB // 2) & (my_y == ny - 1)
    flat_ext[0, rows:ext_rows] = jnp.where(beyond, 0.0, flat_ext[0, rows:ext_rows])

    forcing[...] = surf_in[...]

    depth = flat_ext[0]
    face_levels[0] = jnp.minimum(depth, roll(depth, -1, 1))
    face_levels[1] = jnp.minimum(depth, roll(depth, -1, 0))

    def level(k, carry):
        below = lax.convert_element_type(k, jnp.float32)
        east = jnp.where(face_levels[0] > below, e_ext[k], 0.0)
        nort = jnp.where(face_levels[1] > below, n_ext[k], 0.0)
        current = c_ext[k]
        for _ in range(TSTEPS):
            flux_east = east * jnp.where(east > 0.0, current, roll(current, -1, 1))
            flux_north = nort * jnp.where(nort > 0.0, current, roll(current, -1, 0))
            current = current - (
                flux_east - roll(flux_east, 1, 1) + flux_north - roll(flux_north, 1, 0)
            )
        tracer_out[k] = current[0:rows, 0:cols]
        open_here = flat_ext[0, 0:rows, 0:cols] > below
        forcing[...] += jnp.where(open_here, thickness_ref[k] * current[0:rows, 0:cols], 0.0)
        return carry

    lax.fori_loop(0, levels, level, 0, unroll=2)

    diagonal = 6.0 + flat_ext[1, 0:rows, 0:cols]
    wet = jnp.where(flat_ext[0, 0:rows, 0:cols] > 0.0, 1.0, 0.0)
    z0 = forcing[...] / diagonal
    y0 = wet * z0
    start_vec[0:rows, 0:cols] = y0
    edges = jnp.where(lane_half, y0[:, 0:LANE], y0[:, cols - LANE : cols])
    flat_pack[...] = edges
    edge_pack[...] = edges.T
    last_lanes = pl.ds(LANE - SUB, SUB)
    second = [
        (start_vec.at[last_rows, pl.ds(0, cols)], row_recv.at[0]),
        (start_vec.at[first_rows, pl.ds(0, cols)], row_recv.at[1]),
        (edge_pack.at[last_lanes], edge_recv.at[0]),
        (edge_pack.at[first_rows], edge_recv.at[1]),
        (flat_pack.at[last_rows], edge_corner_recv.at[0]),
        (flat_pack.at[last_rows], edge_corner_recv.at[1]),
        (flat_pack.at[first_rows], edge_corner_recv.at[2]),
        (flat_pack.at[first_rows], edge_corner_recv.at[3]),
    ]
    more = exchange(second, len(AROUND))
    for copy in more:
        copy.wait_recv()

    turned = jnp.concatenate(
        [edge_recv[1], jnp.zeros((LANE - 2 * SUB, rows), jnp.float32), edge_recv[0]], axis=0
    )
    lane_small = iota((SUB, LANE), 1) < LANE // 2
    south = jnp.where(lane_small, edge_corner_recv[1], edge_corner_recv[0])
    north = jnp.where(lane_small, edge_corner_recv[3], edge_corner_recv[2])
    for copy in more:
        copy.wait_send()
    start_vec[0:rows, cols:ext_cols] = turned.T
    start_vec[rows:ext_rows, cols:ext_cols] = jnp.where(small_below, north, south)
    start_vec[rows:ext_rows, 0:cols] = jnp.where(sub < SUB // 2, row_recv[1], row_recv[0])
    start_vec[rows:ext_rows] = jnp.where(beyond, 0.0, start_vec[rows:ext_rows])

    scale = jnp.where(flat_ext[0] > 0.0, 1.0 / (6.0 + flat_ext[1]), 0.0)

    def off_diagonal(vector):
        across = roll(vector, 1, 1) + roll(vector, -1, 1)
        mixed = vector + 0.5 * across
        return scale * (across + roll(mixed, 1, 0) + roll(mixed, -1, 0))

    z1_ext = off_diagonal(start_vec[...])
    z2_ext = off_diagonal(z1_ext)
    z3_ext = off_diagonal(z2_ext)
    z1, z2, z3 = (z[0:rows, 0:cols] for z in (z1_ext, z2_ext, z3_ext))

    def partial(values):
        folded = jnp.sum(values, axis=0, keepdims=True)
        return sum(folded[:, i : i + LANE] for i in range(0, cols, LANE))

    d0, d1, d2 = (diagonal * z for z in (z0, z1, z2))
    sums = [partial(v) for v in (d0 * z0, d0 * z1, d1 * z1, d1 * z2, d2 * z2, d2 * z3)]
    folded = jnp.concatenate(sums + [jnp.zeros((SUB - len(sums), LANE), jnp.float32)], axis=0)
    for shift in (64, 32, 16):
        folded = folded + roll(folded, shift, 1)
    own = iota((SUB, LANE), 1) // (LANE // SUB) == iota((SUB, LANE), 0)
    part[...] = jnp.sum(jnp.where(own, folded, 0.0), axis=0, keepdims=True)

    for offset in range(1, count):
        pltpu.make_async_remote_copy(
            src_ref=part,
            dst_ref=slots.at[offset - 1],
            send_sem=sum_send_sem,
            recv_sem=sum_recv_sem,
            device_id=place(offset),
            device_id_type=MESH,
        ).start()
    everything = pltpu.make_async_remote_copy(
        src_ref=slots,
        dst_ref=slots,
        send_sem=sum_send_sem,
        recv_sem=sum_recv_sem,
        device_id=place(1),
        device_id_type=MESH,
    )
    everything.wait_recv()
    total = jnp.sum(slots[...], axis=0) + part[...]
    total = jnp.sum(jnp.where(own, total, 0.0), axis=1, keepdims=True)
    moment = [total[i : i + 1, :] for i in range(2 * ITERS)]

    def inner(a, b):
        return sum(x * y * moment[i + j] for i, x in enumerate(a) for j, y in enumerate(b))

    def ratio(top, bottom):
        good = bottom > 0.0
        return jnp.where(good, top / jnp.where(good, bottom, 1.0), 0.0)

    one, zero = jnp.ones((1, 1), jnp.float32), jnp.zeros((1, 1), jnp.float32)
    scaled, direction, height = [one], [one], [zero] * ITERS
    product_now = moment[0]
    for iteration in range(ITERS):
        low, high = direction + [zero], [zero] + direction
        applied = [a - b for a, b in zip(low, high)]
        step_size = ratio(product_now, inner(direction, applied))
        for i, x in enumerate(direction):
            height[i] = height[i] + step_size * x
        if iteration + 1 < ITERS:
            scaled = [a - step_size * b for a, b in zip(scaled + [zero], applied)]
            product_next = jnp.maximum(inner(scaled, scaled), 0.0)
            factor = ratio(product_next, product_now)
            direction = [a + factor * b for a, b in zip(scaled, low)]
            product_now = product_next
    heights_out[...] = height[0] * z0 + height[1] * z1 + height[2] * z2

    everything.wait_send()
    for copy in copies:
        copy.wait_send()


def hand_on(tracer_ref, heights_ref, tracer_out, heights_out, save):
    levels = tracer_ref.shape[0]
    stages = [(heights_ref, heights_out)]
    stages += [(tracer_ref.at[k], tracer_out.at[k]) for k in range(levels)]
    saves = [pltpu.make_async_copy(a, b, save.at[i]) for i, (a, b) in enumerate(stages)]
    for copy in saves:
        copy.start()
    for copy in saves:
        copy.wait()


def on_device(ny, nx, tracer, east_speed, north_speed, columns, thickness, surface_flux, helm):
    levels, rows, cols = tracer.shape
    ext = (rows + SUB, cols + LANE)
    hbm = pl.BlockSpec(memory_space=pl.ANY)
    vmem = pl.BlockSpec(memory_space=pltpu.VMEM)
    f32 = jnp.float32
    dma = pltpu.SemaphoreType.DMA
    pairs = pl.cdiv(4 * (3 * levels + 2), 2 * SUB)
    scratch = [
        pltpu.VMEM((levels, *ext), f32),
        pltpu.VMEM((levels, *ext), f32),
        pltpu.VMEM((levels, *ext), f32),
        pltpu.VMEM((rows, cols), jnp.int32),
        pltpu.VMEM((rows, cols), f32),
        pltpu.VMEM((2, *ext), f32),
        pltpu.VMEM((2, *ext), f32),
        pltpu.VMEM((rows, LANE), f32),
        *[pltpu.VMEM((pairs, SUB, rows), f32)] * 4,
        pltpu.VMEM((4, SUB, LANE), f32),
        pltpu.VMEM((levels, SUB, cols), f32),
        pltpu.VMEM((levels, SUB, cols), f32),
        pltpu.VMEM((levels, SUB, cols), f32),
        pltpu.VMEM((levels, SUB, cols), f32),
        pltpu.VMEM((rows, cols), f32),
        pltpu.VMEM(ext, f32),
        pltpu.VMEM((rows, LANE), f32),
        pltpu.VMEM((LANE, rows), f32),
        pltpu.VMEM((2, SUB, cols), f32),
        pltpu.VMEM((2, SUB, rows), f32),
        pltpu.VMEM((4, SUB, LANE), f32),
        pltpu.VMEM((1, LANE), f32),
        pltpu.VMEM((ny * nx - 1, 1, LANE), f32),
        pltpu.SMEM((levels,), f32),
        dma((7,)),
        dma,
        dma((2 * len(AROUND),)),
        dma((2 * len(AROUND),)),
        dma,
        dma,
    ]
    results = pl.pallas_call(
        functools.partial(kernel, ny, nx),
        out_shape=(
            pltpu.VMEM((levels, rows, cols), f32),
            pltpu.VMEM((rows, cols), f32),
        ),
        in_specs=[hbm, hbm, hbm, hbm, hbm, hbm, hbm],
        out_specs=(vmem, vmem),
        scratch_shapes=scratch,
        compiler_params=pltpu.CompilerParams(collective_id=0, has_side_effects=True),
    )(tracer, east_speed, north_speed, columns, thickness, surface_flux, helm)
    return pl.pallas_call(
        hand_on,
        out_shape=tuple(jax.ShapeDtypeStruct(r.shape, f32) for r in results),
        in_specs=[vmem, vmem],
        out_specs=(hbm, hbm),
        scratch_shapes=[dma((levels + 1,))],
    )(*[pltpu.with_memory_space_constraint(r, pltpu.VMEM) for r in results])


def solution(mesh):
    spec = P(None, "gy", "gx")
    flat = P("gy", "gx")
    return jax.shard_map(
        functools.partial(on_device, mesh.shape["gy"], mesh.shape["gx"]),
        mesh=mesh,
        in_specs=(spec, spec, spec, flat, P(), flat, flat),
        out_specs=(spec, flat),
        check_vma=False,
    )
```

profile of v0, /device:TPU:0, one launch (start us, length us, event | category | flops | bytes accessed | tf_op | source)
XLA Modules:
  0.0 26.1 jit_solution(12907122142424147940)
XLA Ops:
  0.6 24.4 %shard_map.86 = (f32[8,128,256]{2,1,0:T(8,128)S(1)}, f32[128,256]{1,0:T(8,128)S(1)}) custom-call(f32[8,128,256]{2,1,0:T(8,128)} %tracer_ref.1, f32[8,128,256]{2,1,0:T(8,128)} %east_ref.1, f32[8,128,256]{2,1,0:T(8,128)} %north_ref.1, s32[128,256]{1,0:T(8,128)} %columns_ref.1, f32[8]{0:T(128)} %thick_hbm.1, f32[128,256]{1,0:T(8,128)} %surface_ref.1, ...), custom_call_target="tpu_custom_call" | custom-call | tf_op jit(solution)/shard_map/pallas_call | solution.py:389
  25.0 1.1 %shard_map.87 = (f32[8,128,256]{2,1,0:T(8,128)}, f32[128,256]{1,0:T(8,128)}) custom-call(f32[8,128,256]{2,1,0:T(8,128)S(1)} %get-tuple-element.4.tracer_ref, f32[128,256]{1,0:T(8,128)S(1)} %get-tuple-element.5.heights_ref), custom_call_target="tpu_custom_call" | custom-call | tf_op jit(solution)/shard_map/pallas_call | solution.py:400
where the time goes:
time: 26.2 us; the launch traced here: 26.1 us
  Pallas kernels  25.4 us (97%)
  between operations  0.64 us (2%)
    pallas_call x1, Pallas kernels, on_device(): pl.pallas_call(functools.partial(kernel, ny, nx), out_shape=(pltpu.VMEM((...  24.4 us
    pallas_call x1, Pallas kernels, on_device(): pl.pallas_call(hand_on, out_shape=tuple((jax.ShapeDtypeStruct(r.shape, f3...  1.08 us

commit v1 on v0

v1 whole, which is shorter than its diff:
```python
import functools

import jax
import jax.numpy as jnp
from jax import lax
from jax.experimental import pallas as pl
from jax.experimental.pallas import tpu as pltpu
from jax.sharding import PartitionSpec as P

TSTEPS = 2
ITERS = 3
MESH = pl.DeviceIdType.MESH
SUB = 8
LANE = 128
SEAM = 16


def roll(array, shift, axis):
    shift = shift % array.shape[axis]
    return pltpu.roll(array, shift, axis) if shift else array


def iota(shape, dim):
    return lax.broadcasted_iota(jnp.int32, shape, dim)


def pick(array, lanes):
    return jnp.take_along_axis(array, lanes, axis=1, mode="promise_in_bounds")


def transport(current, east, nort, open_east, open_nort):
    east = jnp.where(open_east, east, 0.0)
    nort = jnp.where(open_nort, nort, 0.0)
    for _ in range(TSTEPS):
        flux_east = east * jnp.where(east > 0.0, current, roll(current, -1, 1))
        flux_north = nort * jnp.where(nort > 0.0, current, roll(current, -1, 0))
        current = current - (flux_east - roll(flux_east, 1, 1) + flux_north - roll(flux_north, 1, 0))
    return current


def kernel(
    ny,
    nx,
    tracer_ref,
    east_ref,
    north_ref,
    columns_ref,
    thick_hbm,
    surface_ref,
    helm_ref,
    tracer_out,
    heights_out,
    fields,
    col_in,
    flat_ext,
    own_tile,
    to_east,
    to_west,
    from_west,
    from_east,
    corner,
    rows_up,
    rows_down,
    rows_south,
    rows_north,
    flat_up,
    flat_down,
    flat_south,
    flat_north,
    tile_south,
    tile_north,
    strip_south,
    strip_north,
    level_sum,
    faces,
    part,
    slots,
    thickness,
    in_sem,
    send_sem,
    recv_sem,
    sum_send_sem,
    sum_recv_sem,
):
    _, levels, rows, cols = fields.shape
    my_y, my_x = lax.axis_index("gy"), lax.axis_index("gx")
    count = ny * nx

    def wrap(value, size):
        return jnp.where(value >= size, value - size, value)

    ys = [my_y] + [wrap(my_y + d, ny) for d in range(1, ny)]
    xs = [my_x] + [wrap(my_x + d, nx) for d in range(1, nx)]
    others = [(y, x) for b, x in enumerate(xs) for a, y in enumerate(ys) if a or b]
    south_here, north_here = my_y > 0, my_y < ny - 1

    small = [
        pltpu.make_async_copy(columns_ref, col_in, in_sem.at[0]),
        pltpu.make_async_copy(helm_ref, flat_ext.at[1, 0:rows, 0:cols], in_sem.at[1]),
        pltpu.make_async_copy(surface_ref, flat_ext.at[2, 0:rows, 0:cols], in_sem.at[2]),
    ]
    large = [
        pltpu.make_async_copy(ref, fields.at[f], in_sem.at[3 + f])
        for f, ref in enumerate((tracer_ref, east_ref, north_ref))
    ]
    thick = pltpu.make_async_copy(thick_hbm, thickness, in_sem.at[6])
    for load in small + large + [thick]:
        load.start()
    barrier = pltpu.get_barrier_semaphore()
    for target in reversed(others):
        pl.semaphore_signal(barrier, inc=1, device_id=target, device_id_type=MESH)

    lane = iota((rows, LANE), 1)
    group = lane // SEAM
    seat = lane % SEAM
    first_rows, last_rows = pl.ds(0, SUB), pl.ds(rows - SUB, SUB)

    def both_edges(left, right):
        return jnp.where(lane < LANE // 2, left, right)

    def flat_edges(f):
        return both_edges(flat_ext[f, 0:rows, 0:LANE], flat_ext[f, 0:rows, cols - LANE : cols])

    def spare_lane(slot):
        return SEAM * (slot // 2) + SEAM - 2 + slot % 2

    for load in small:
        load.wait()
    flat_ext[0, 0:rows, 0:cols] = col_in[...].astype(jnp.float32)
    depth_edge = flat_edges(0)
    own_tile[3] = pick(depth_edge, (LANE - SUB + seat) % LANE)
    three = jnp.where(
        (lane < SUB) | (lane >= LANE - SUB),
        depth_edge,
        jnp.where(lane < 3 * SUB, roll(flat_edges(1), 2 * SUB, 1), roll(flat_edges(2), 4 * SUB, 1)),
    )
    slot = jnp.maximum(2 * group + seat - (SEAM - 2), 0)
    east_from = jnp.where(slot < 6, LANE - 5 + slot, jnp.where(slot < 10, slot - 6 + 13, slot - 10 + 29)) % LANE
    west_from = jnp.where(slot < 6, slot, jnp.where(slot < 10, slot - 6 + 16, slot - 10 + 32)) % LANE
    spare_east, spare_west = pick(three, east_from), pick(three, west_from)
    for f in range(3):
        flat_up[f] = flat_ext[f, rows - SUB : rows, 0:cols]
        flat_down[f] = flat_ext[f, 0:SUB, 0:cols]

    tiles = []
    for f in range(3):
        large[f].wait()
        packed = None
        for k in range(levels):
            moved = roll(both_edges(fields[f, k, :, 0:LANE], fields[f, k, :, cols - LANE : cols]), SEAM * k + SUB, 1)
            packed = moved if packed is None else jnp.where(group == k, moved, packed)
        own_tile[f] = packed
        tiles.append(packed)

    def message(shifts, spare):
        c, e, n = (roll(tile, shift, 1) for tile, shift in zip(tiles, shifts))
        return jnp.where(seat < 5, c, jnp.where(seat < 10, e, jnp.where(seat < SEAM - 2, n, spare)))

    to_east[...] = message((-3, 2, 6), spare_east)
    to_west[...] = message((-8, -3, 2), spare_west)

    sub = iota((SUB, cols), 0)
    for k in range(levels):
        c, e, n = (fields[f, k, rows - SUB : rows] for f in range(3))
        rows_up[k, 0:SUB] = jnp.where(sub < 3, roll(n, -3, 0), c)
        rows_up[k, SUB : 2 * SUB] = jnp.where(sub < 4, roll(n, 2, 0), e)
        c, e, n = (fields[f, k, 0:SUB] for f in range(3))
        rows_down[k, 0:SUB] = jnp.where(sub < 5, c, roll(n, 5, 0))
        rows_down[k, SUB : 2 * SUB] = jnp.where(sub < 4, e, roll(n, 1, 0))

    pl.semaphore_wait(barrier, count - 1)

    up, down, right, left = wrap(my_y + 1, ny), wrap(my_y + ny - 1, ny), xs[1], xs[-1]
    plan = [
        (to_east, from_west, (my_y, right)),
        (to_west, from_east, (my_y, left)),
        (rows_up, rows_south, (up, my_x)),
        (flat_up, flat_south, (up, my_x)),
        (own_tile.at[:, last_rows], tile_south, (up, my_x)),
        (to_east.at[last_rows], corner.at[0], (up, right)),
        (to_west.at[last_rows], corner.at[2], (up, left)),
        (rows_down, rows_north, (down, my_x)),
        (flat_down, flat_north, (down, my_x)),
        (own_tile.at[:, first_rows], tile_north, (down, my_x)),
        (to_east.at[first_rows], corner.at[1], (down, right)),
        (to_west.at[first_rows], corner.at[3], (down, left)),
    ]
    copies = [
        pltpu.make_async_remote_copy(
            src_ref=source,
            dst_ref=target,
            send_sem=send_sem.at[which],
            recv_sem=recv_sem.at[which],
            device_id=device,
            device_id_type=MESH,
        )
        for which, (source, target, device) in enumerate(plan)
    ]
    beside, upward, downward = copies[0:2], copies[2:7], copies[7:12]

    def each(items, act):
        for item in items:
            act(item)

    start, wait_recv, wait_send = (lambda c: c.start()), (lambda c: c.wait_recv()), (lambda c: c.wait_send())
    pl.when(north_here)(lambda: each(upward[3:], start))
    pl.when(south_here)(lambda: each(downward[3:], start))
    each(beside, start)
    pl.when(north_here)(lambda: each(upward[:3], start))
    pl.when(south_here)(lambda: each(downward[:3], start))

    thick.wait()
    depth = flat_ext[0, 0:rows, 0:cols]
    faces[0] = jnp.minimum(depth, roll(depth, -1, 1))
    faces[1] = jnp.minimum(depth, roll(depth, -1, 0))
    level_sum[0:rows, 0:cols] = jnp.zeros((rows, cols), jnp.float32)

    def level(k, carry):
        below = lax.convert_element_type(k, jnp.float32)
        current = transport(fields[0, k], fields[1, k], fields[2, k], faces[0] > below, faces[1] > below)
        tracer_out[k] = current
        open_here = flat_ext[0, 0:rows, 0:cols] > below
        level_sum[0:rows, 0:cols] += jnp.where(open_here, thickness[k] * current, 0.0)
        return carry

    lax.fori_loop(0, levels, level, 0, unroll=2)

    @pl.when(jnp.logical_not(south_here))
    def _():
        for ref in (rows_south, flat_south, tile_south):
            ref[...] = jnp.zeros(ref.shape, jnp.float32)
        for which in (0, 2):
            corner[which] = jnp.zeros((SUB, LANE), jnp.float32)

    @pl.when(jnp.logical_not(north_here))
    def _():
        for ref in (rows_north, flat_north, tile_north):
            ref[...] = jnp.zeros(ref.shape, jnp.float32)
        for which in (1, 3):
            corner[which] = jnp.zeros((SUB, LANE), jnp.float32)

    pl.when(south_here)(lambda: each(upward[:3], wait_recv))
    pl.when(north_here)(lambda: each(downward[:3], wait_recv))

    stacked_level = (iota((2 * SUB * levels, cols), 0) // (2 * SUB)).astype(jnp.float32)

    def row_strip(pieces, depth16, out):
        c, e, n = (jnp.concatenate(p, axis=0) for p in pieces)
        deep = jnp.concatenate([depth16] * levels, axis=0)
        open_east = jnp.minimum(deep, roll(deep, -1, 1)) > stacked_level
        open_nort = jnp.minimum(deep, roll(deep, -1, 0)) > stacked_level
        new = transport(c, e, n, open_east, open_nort)
        out[...] = new
        total = None
        for k in range(levels):
            term = jnp.where(depth16 > k, thickness[k] * new[2 * SUB * k : 2 * SUB * (k + 1)], 0.0)
            total = term if total is None else total + term
        return total

    south, north = ([], [], []), ([], [], [])
    for k in range(levels):
        a, b = rows_south[k, 0:SUB], rows_south[k, SUB : 2 * SUB]
        for f, halo in enumerate((a, b, jnp.where(sub < 6, roll(a, 3, 0), roll(b, -2, 0)))):
            south[f].extend([halo, fields[f, k, 0:SUB]])
        a, b = rows_north[k, 0:SUB], rows_north[k, SUB : 2 * SUB]
        for f, halo in enumerate((a, b, jnp.where(sub < 3, roll(a, -5, 0), roll(b, -1, 0)))):
            north[f].extend([fields[f, k, rows - SUB : rows], halo])
    sum_south = row_strip(south, jnp.concatenate([flat_south[0], flat_down[0]], axis=0), strip_south)
    sum_north = row_strip(north, jnp.concatenate([flat_up[0], flat_north[0]], axis=0), strip_north)
    level_sum[0:SUB, 0:cols] = jnp.where(sub < 2, sum_south[SUB:], level_sum[0:SUB, 0:cols])
    level_sum[rows - SUB : rows, 0:cols] = jnp.where(
        sub >= SUB - 2, sum_north[0:SUB], level_sum[rows - SUB : rows, 0:cols]
    )
    level_sum[rows : rows + SUB, 0:cols] = jnp.where(sub < SUB // 2, sum_north[SUB:], sum_south[0:SUB])
    for f in range(3):
        flat_ext[f, rows : rows + SUB, 0:cols] = jnp.where(sub < SUB // 2, flat_north[f], flat_south[f])

    tall = rows + 2 * SUB
    lane = iota((tall, LANE), 1)
    group = lane // SEAM
    seat = lane % SEAM
    strip_level = group.astype(jnp.float32)
    lane_thickness = jnp.zeros((tall, LANE), jnp.float32)
    for k in range(levels):
        lane_thickness = jnp.where(group == k, thickness[k], lane_thickness)
    own = [
        jnp.concatenate([tile_south[f], own_tile[f], tile_north[f]], axis=0) for f in range(4)
    ]
    low_seat = seat < SUB
    small_sub = iota((SUB, LANE), 0) < SUB // 2

    each(beside, wait_recv)
    pl.when(south_here)(lambda: each(upward[3:], wait_recv))
    pl.when(north_here)(lambda: each(downward[3:], wait_recv))

    def cyclic(array):
        turn = jnp.where(small_sub, array[rows + SUB :], array[0:SUB])
        return jnp.concatenate([array[SUB : rows + SUB], turn], axis=0)

    west = jnp.concatenate([corner[0], from_west[...], corner[1]], axis=0)
    east = jnp.concatenate([corner[2], from_east[...], corner[3]], axis=0)

    def side_strip(got, shifts, first, halo_seat):
        slots_of = jnp.minimum(jnp.maximum(seat - first, 0), 4)
        got_c, got_e, got_n = (roll(got, shift, 1) for shift in shifts)
        got_d = pick(got, spare_lane(slots_of))
        c, e, n, d = (jnp.where(halo_seat, g, o) for g, o in zip((got_c, got_e, got_n, got_d), own))
        open_east = jnp.minimum(d, roll(d, -1, 1)) > strip_level
        open_nort = jnp.minimum(d, roll(d, -1, 0)) > strip_level
        new = transport(c, e, n, open_east, open_nort)
        total = jnp.where(d > strip_level, lane_thickness * new, 0.0)
        for shift in (64, 32, 16):
            total = total + roll(total, shift, 1)
        return new, cyclic(roll(total, -SUB, 1))

    new_west, sum_west = side_strip(west, (3, -2, -6), 3, low_seat)
    new_east, sum_east = side_strip(east, (8, 3, -2), 8, jnp.logical_not(low_seat))

    flat_lane = iota((rows + SUB, LANE), 1)
    half = flat_lane < LANE // 2
    level_sum[:, cols : cols + LANE] = jnp.where(half, sum_east, sum_west)
    level_sum[:, 0:LANE] = jnp.where(flat_lane < 2, sum_west, level_sum[:, 0:LANE])
    level_sum[:, cols - LANE : cols] = jnp.where(flat_lane >= LANE - 2, sum_east, level_sum[:, cols - LANE : cols])
    for f, (base_west, base_east) in enumerate(((2, 0), (6, 6), (10, 10))):
        from_slot = jnp.where(lane < LANE // 2, base_east + (lane & 3), base_west + ((lane - (LANE - 3)) & 3))
        seen = spare_lane(from_slot)
        side = jnp.where(lane < LANE // 2, pick(east, seen), pick(west, seen))
        flat_ext[f, :, cols : cols + LANE] = cyclic(side)

    deep = flat_ext[0]
    inverse = 1.0 / (6.0 + flat_ext[1])
    wet = deep > 0.0
    scale = jnp.where(wet, inverse, 0.0)
    z0_ext = (flat_ext[2] + level_sum[...]) * inverse
    start_vec = jnp.where(wet, z0_ext, 0.0)

    def off_diagonal(vector):
        across = roll(vector, 1, 1) + roll(vector, -1, 1)
        mixed = vector + 0.5 * across
        return scale * (across + roll(mixed, 1, 0) + roll(mixed, -1, 0))

    z1_ext = off_diagonal(start_vec)
    z2_ext = off_diagonal(z1_ext)
    z3_ext = off_diagonal(z2_ext)
    z0, z1, z2, z3 = (z[0:rows, 0:cols] for z in (z0_ext, z1_ext, z2_ext, z3_ext))
    diagonal = 6.0 + flat_ext[1, 0:rows, 0:cols]

    def partial(values):
        folded = jnp.sum(values, axis=0, keepdims=True)
        return sum(folded[:, i : i + LANE] for i in range(0, cols, LANE))

    d0, d1, d2 = (diagonal * z for z in (z0, z1, z2))
    sums = [partial(v) for v in (d0 * z0, d0 * z1, d1 * z1, d1 * z2, d2 * z2, d2 * z3)]
    folded = jnp.concatenate(sums + [jnp.zeros((SUB - len(sums), LANE), jnp.float32)], axis=0)
    for shift in (64, 32, 16):
        folded = folded + roll(folded, shift, 1)
    diag = iota((SUB, LANE), 1) // (LANE // SUB) == iota((SUB, LANE), 0)
    part[...] = jnp.sum(jnp.where(diag, folded, 0.0), axis=0, keepdims=True)

    for index, target in enumerate(others):
        pltpu.make_async_remote_copy(
            src_ref=part,
            dst_ref=slots.at[index],
            send_sem=sum_send_sem,
            recv_sem=sum_recv_sem,
            device_id=target,
            device_id_type=MESH,
        ).start()

    for k in range(levels):
        tracer_out[k, 0:SUB] = jnp.where(sub < 2, strip_south[2 * SUB * k + SUB : 2 * SUB * (k + 1)], tracer_out[k, 0:SUB])
        tracer_out[k, rows - SUB : rows] = jnp.where(
            sub >= SUB - 2, strip_north[2 * SUB * k : 2 * SUB * k + SUB], tracer_out[k, rows - SUB : rows]
        )
    side_new = jnp.where(low_seat, new_east, new_west)[SUB : rows + SUB]
    lane = iota((rows, LANE), 1)
    for k in range(levels):
        moved = roll(side_new, -SEAM * k - SUB, 1)
        tracer_out[k, :, 0:LANE] = jnp.where(lane < 2, moved, tracer_out[k, :, 0:LANE])
        tracer_out[k, :, cols - LANE : cols] = jnp.where(lane >= LANE - 2, moved, tracer_out[k, :, cols - LANE : cols])

    everything = pltpu.make_async_remote_copy(
        src_ref=slots,
        dst_ref=slots,
        send_sem=sum_send_sem,
        recv_sem=sum_recv_sem,
        device_id=others[0],
        device_id_type=MESH,
    )
    everything.wait_recv()
    total = jnp.sum(slots[...], axis=0) + part[...]
    total = jnp.sum(jnp.where(diag, total, 0.0), axis=1, keepdims=True)
    moment = [total[i : i + 1, :] for i in range(2 * ITERS)]

    def inner(a, b):
        return sum(x * y * moment[i + j] for i, x in enumerate(a) for j, y in enumerate(b))

    def ratio(top, bottom):
        good = bottom > 0.0
        return jnp.where(good, top / jnp.where(good, bottom, 1.0), 0.0)

    one, zero = jnp.ones((1, 1), jnp.float32), jnp.zeros((1, 1), jnp.float32)
    scaled, direction, height = [one], [one], [zero] * ITERS
    product_now = moment[0]
    for iteration in range(ITERS):
        low, high = direction + [zero], [zero] + direction
        applied = [a - b for a, b in zip(low, high)]
        step_size = ratio(product_now, inner(direction, applied))
        for i, x in enumerate(direction):
            height[i] = height[i] + step_size * x
        if iteration + 1 < ITERS:
            scaled = [a - step_size * b for a, b in zip(scaled + [zero], applied)]
            product_next = jnp.maximum(inner(scaled, scaled), 0.0)
            factor = ratio(product_next, product_now)
            direction = [a + factor * b for a, b in zip(scaled, low)]
            product_now = product_next
    heights_out[...] = height[0] * z0 + height[1] * z1 + height[2] * z2

    everything.wait_send()
    each(beside, wait_send)
    pl.when(north_here)(lambda: each(upward, wait_send))
    pl.when(south_here)(lambda: each(downward, wait_send))


def hand_on(tracer_ref, heights_ref, tracer_out, heights_out, save):
    levels = tracer_ref.shape[0]
    stages = [(heights_ref, heights_out)]
    stages += [(tracer_ref.at[k], tracer_out.at[k]) for k in range(levels)]
    saves = [pltpu.make_async_copy(a, b, save.at[i]) for i, (a, b) in enumerate(stages)]
    for copy in saves:
        copy.start()
    for copy in saves:
        copy.wait()


def on_device(ny, nx, tracer, east_speed, north_speed, columns, thickness, surface_flux, helm):
    levels, rows, cols = tracer.shape
    ext = (rows + SUB, cols + LANE)
    hbm = pl.BlockSpec(memory_space=pl.ANY)
    vmem = pl.BlockSpec(memory_space=pltpu.VMEM)
    f32 = jnp.float32
    dma = pltpu.SemaphoreType.DMA
    scratch = [
        pltpu.VMEM((3, levels, rows, cols), f32),
        pltpu.VMEM((rows, cols), jnp.int32),
        pltpu.VMEM((3, *ext), f32),
        pltpu.VMEM((4, rows, LANE), f32),
        *[pltpu.VMEM((rows, LANE), f32)] * 4,
        pltpu.VMEM((4, SUB, LANE), f32),
        *[pltpu.VMEM((levels, 2 * SUB, cols), f32)] * 4,
        *[pltpu.VMEM((3, SUB, cols), f32)] * 4,
        *[pltpu.VMEM((4, SUB, LANE), f32)] * 2,
        *[pltpu.VMEM((levels * 2 * SUB, cols), f32)] * 2,
        pltpu.VMEM(ext, f32),
        pltpu.VMEM((2, rows, cols), f32),
        pltpu.VMEM((1, LANE), f32),
        pltpu.VMEM((ny * nx - 1, 1, LANE), f32),
        pltpu.SMEM((levels,), f32),
        dma((7,)),
        dma((12,)),
        dma((12,)),
        dma,
        dma,
    ]
    results = pl.pallas_call(
        functools.partial(kernel, ny, nx),
        out_shape=(
            pltpu.VMEM((levels, rows, cols), f32),
            pltpu.VMEM((rows, cols), f32),
        ),
        in_specs=[hbm] * 7,
        out_specs=(vmem, vmem),
        scratch_shapes=scratch,
        compiler_params=pltpu.CompilerParams(collective_id=0, has_side_effects=True),
    )(tracer, east_speed, north_speed, columns, thickness, surface_flux, helm)
    return pl.pallas_call(
        hand_on,
        out_shape=tuple(jax.ShapeDtypeStruct(r.shape, f32) for r in results),
        in_specs=[vmem, vmem],
        out_specs=(hbm, hbm),
        scratch_shapes=[dma((levels + 1,))],
    )(*[pltpu.with_memory_space_constraint(r, pltpu.VMEM) for r in results])


def solution(mesh):
    spec = P(None, "gy", "gx")
    flat = P("gy", "gx")
    return jax.shard_map(
        functools.partial(on_device, mesh.shape["gy"], mesh.shape["gx"]),
        mesh=mesh,
        in_specs=(spec, spec, spec, flat, P(), flat, flat),
        out_specs=(spec, flat),
        check_vma=False,
    )
```

time: 26.2 us -> 20.8 us (0.79)
  Pallas kernels: 25.4 us -> 20 us
    pallas_call x1, Pallas kernels: 24.4 us -> 18.9 us  [on_device(): pl.pallas_call(functools.partial(kernel, ny, nx), out_shape=(pltpu.VMEM((...]
where the time goes in v1:
time: 20.8 us; the launch traced here: 20.6 us
  Pallas kernels  20 us (96%)
  between operations  0.64 us (3%)
    pallas_call x1, Pallas kernels, on_device(): pl.pallas_call(functools.partial(kernel, ny, nx), out_shape=(pltpu.VMEM((...  18.9 us
    pallas_call x1, Pallas kernels, on_device(): pl.pallas_call(hand_on, out_shape=tuple((jax.ShapeDtypeStruct(r.shape, f3...  1.08 us

profile of v1, /device:TPU:0, one launch (start us, length us, event | category | flops | bytes accessed | tf_op | source)
XLA Modules:
  0.0 20.6 jit_solution(18215348012268709147)
XLA Ops:
  0.6 18.9 %shard_map.86 = (f32[8,128,256]{2,1,0:T(8,128)S(1)}, f32[128,256]{1,0:T(8,128)S(1)}) custom-call(f32[8,128,256]{2,1,0:T(8,128)} %tracer_ref.1, f32[8,128,256]{2,1,0:T(8,128)} %east_ref.1, f32[8,128,256]{2,1,0:T(8,128)} %north_ref.1, s32[128,256]{1,0:T(8,128)} %columns_ref.1, f32[8]{0:T(128)} %thick_hbm.1, f32[128,256]{1,0:T(8,128)} %surface_ref.1, ...), custom_call_target="tpu_custom_call" | custom-call | tf_op jit(solution)/shard_map/pallas_call | solution.py:465
  19.6 1.1 %shard_map.87 = (f32[8,128,256]{2,1,0:T(8,128)}, f32[128,256]{1,0:T(8,128)}) custom-call(f32[8,128,256]{2,1,0:T(8,128)S(1)} %get-tuple-element.4.tracer_ref, f32[128,256]{1,0:T(8,128)S(1)} %get-tuple-element.5.heights_ref), custom_call_target="tpu_custom_call" | custom-call | tf_op jit(solution)/shard_map/pallas_call | solution.py:476

commit v2 on v1

v2 whole, which is shorter than its diff:
```python
import functools

import jax
import jax.numpy as jnp
from jax import lax
from jax.experimental import pallas as pl
from jax.experimental.pallas import tpu as pltpu
from jax.sharding import PartitionSpec as P

TSTEPS = 2
ITERS = 3
MESH = pl.DeviceIdType.MESH
SUB = 8
LANE = 128
SEAM = 16


def roll(array, shift, axis):
    shift = shift % array.shape[axis]
    return pltpu.roll(array, shift, axis) if shift else array


def iota(shape, dim):
    return lax.broadcasted_iota(jnp.int32, shape, dim)


def pick(array, lanes):
    return jnp.take_along_axis(array, lanes, axis=1, mode="promise_in_bounds")


def transport(current, east, nort, open_east, open_nort):
    east = jnp.where(open_east, east, 0.0)
    nort = jnp.where(open_nort, nort, 0.0)
    for _ in range(TSTEPS):
        flux_east = east * jnp.where(east > 0.0, current, roll(current, -1, 1))
        flux_north = nort * jnp.where(nort > 0.0, current, roll(current, -1, 0))
        current = current - (flux_east - roll(flux_east, 1, 1) + flux_north - roll(flux_north, 1, 0))
    return current


def kernel(
    ny,
    nx,
    tracer_ref,
    east_ref,
    north_ref,
    columns_ref,
    thick_hbm,
    surface_ref,
    helm_ref,
    tracer_out,
    basis_out,
    moments_out,
    fields,
    col_in,
    flat,
    own_tile,
    to_east,
    to_west,
    west,
    east,
    rows_up,
    rows_down,
    rows_south,
    rows_north,
    strip_south,
    strip_north,
    own_sum,
    faces,
    strips,
    level_sum,
    scale,
    start_vec,
    part,
    slots,
    thickness,
    know_sem,
    in_sem,
    send_sem,
    recv_sem,
    sum_send_sem,
    sum_recv_sem,
):
    _, levels, rows, cols = fields.shape
    my_y, my_x = lax.axis_index("gy"), lax.axis_index("gx")

    def wrap(value, size):
        return jnp.where(value >= size, value - size, value)

    ys = [my_y] + [wrap(my_y + d, ny) for d in range(1, ny)]
    xs = [my_x] + [wrap(my_x + d, nx) for d in range(1, nx)]
    others = [(y, x) for b, x in enumerate(xs) for a, y in enumerate(ys) if a or b]
    south_here, north_here = my_y > 0, my_y < ny - 1

    blocks = range(cols // LANE)
    side_block = cols // LANE
    inside = pl.ds(SUB, rows)
    small = [pltpu.make_async_copy(columns_ref, col_in, in_sem.at[0])] + [
        pltpu.make_async_copy(ref.at[:, pl.ds(LANE * b, LANE)], flat.at[f, b, inside], in_sem.at[7 + len(blocks) * (f - 1) + b])
        for f, ref in ((1, helm_ref), (2, surface_ref))
        for b in blocks
    ]
    large = [
        pltpu.make_async_copy(ref, fields.at[f], in_sem.at[3 + f])
        for f, ref in enumerate((tracer_ref, east_ref, north_ref))
    ]
    thick = pltpu.make_async_copy(thick_hbm, thickness, in_sem.at[6])
    for load in small + large + [thick]:
        load.start()
    barrier = pltpu.get_barrier_semaphore()

    def around(reach_y, reach_x):
        return [(ys[a], xs[b]) for a in reach_y for b in reach_x if a or b]

    def reach(distance, known, size):
        return (0,) if 2 * known + 1 >= size else (distance, -distance, 0)

    greeted = around(reach(1, 0, ny), reach(1, 0, nx))
    for target in greeted:
        pl.semaphore_signal(barrier, inc=1, device_id=target, device_id_type=MESH)
    rounds, known = [], 1
    while 2 * known + 1 < max(ny, nx):
        rounds.append(around(reach(known, known, ny), reach(known, known, nx)))
        known *= 2

    def tell(turn):
        for target in rounds[turn]:
            pl.semaphore_signal(know_sem.at[turn], inc=1, device_id=target, device_id_type=MESH)

    def hear(turn):
        pl.semaphore_wait(know_sem.at[turn], len(rounds[turn]))


    lane = iota((rows, LANE), 1)
    group = lane // SEAM
    seat = lane % SEAM
    first_rows, last_rows = pl.ds(0, SUB), pl.ds(rows - SUB, SUB)
    low_halo, low_own, high_own, high_halo = (pl.ds(at, SUB) for at in (0, SUB, rows, rows + SUB))

    def both_edges(left, right):
        return jnp.where(lane < LANE // 2, left, right)

    def flat_edges(f):
        return both_edges(flat[f, 0, inside], flat[f, side_block - 1, inside])

    def spare_lane(slot):
        return SEAM * (slot // 2) + SEAM - 2 + slot % 2

    for load in small:
        load.wait()
    for b in blocks:
        flat[0, b, inside] = col_in[:, LANE * b : LANE * (b + 1)].astype(jnp.float32)
    depth_edge = flat_edges(0)
    own_tile[3, inside] = pick(depth_edge, (LANE - SUB + seat) % LANE)
    three = jnp.where(
        (lane < SUB) | (lane >= LANE - SUB),
        depth_edge,
        jnp.where(lane < 3 * SUB, roll(flat_edges(1), 2 * SUB, 1), roll(flat_edges(2), 4 * SUB, 1)),
    )
    slot = jnp.maximum(2 * group + seat - (SEAM - 2), 0)
    east_from = jnp.where(slot < 6, LANE - 5 + slot, jnp.where(slot < 10, slot - 6 + 13, slot - 10 + 29)) % LANE
    west_from = jnp.where(slot < 6, slot, jnp.where(slot < 10, slot - 6 + 16, slot - 10 + 32)) % LANE
    spare_east, spare_west = pick(three, east_from), pick(three, west_from)
    tiles = []
    for f in range(3):
        large[f].wait()
        packed = None
        for k in range(levels):
            moved = roll(both_edges(fields[f, k, :, 0:LANE], fields[f, k, :, cols - LANE : cols]), SEAM * k + SUB, 1)
            packed = moved if packed is None else jnp.where(group == k, moved, packed)
        own_tile[f, inside] = packed
        tiles.append(packed)

    def message(shifts, spare):
        c, e, n = (roll(tile, shift, 1) for tile, shift in zip(tiles, shifts))
        return jnp.where(seat < 5, c, jnp.where(seat < 10, e, jnp.where(seat < SEAM - 2, n, spare)))

    to_east[...] = message((-3, 2, 6), spare_east)
    to_west[...] = message((-8, -3, 2), spare_west)

    sub = iota((SUB, cols), 0)
    for k in range(levels):
        c, e, n = (fields[f, k, rows - SUB : rows] for f in range(3))
        rows_up[k, 0:SUB] = jnp.where(sub < 3, roll(n, -3, 0), c)
        rows_up[k, SUB : 2 * SUB] = jnp.where(sub < 4, roll(n, 2, 0), e)
        c, e, n = (fields[f, k, 0:SUB] for f in range(3))
        rows_down[k, 0:SUB] = jnp.where(sub < 5, c, roll(n, 5, 0))
        rows_down[k, SUB : 2 * SUB] = jnp.where(sub < 4, e, roll(n, 1, 0))

    pl.semaphore_wait(barrier, len(greeted))

    up, down, right, left = wrap(my_y + 1, ny), wrap(my_y + ny - 1, ny), xs[1], xs[-1]
    body = pl.ds(0, side_block)
    plan = [
        (to_east, west.at[inside], (my_y, right)),
        (to_west, east.at[inside], (my_y, left)),
        (rows_up, rows_south, (up, my_x)),
        (flat.at[:, body, high_own], flat.at[:, body, low_halo], (up, my_x)),
        (own_tile.at[:, high_own], own_tile.at[:, low_halo], (up, my_x)),
        (to_east.at[last_rows], west.at[low_halo], (up, right)),
        (to_west.at[last_rows], east.at[low_halo], (up, left)),
        (rows_down, rows_north, (down, my_x)),
        (flat.at[:, body, low_own], flat.at[:, body, high_halo], (down, my_x)),
        (own_tile.at[:, low_own], own_tile.at[:, high_halo], (down, my_x)),
        (to_east.at[first_rows], west.at[high_halo], (down, right)),
        (to_west.at[first_rows], east.at[high_halo], (down, left)),
    ]
    copies = [
        pltpu.make_async_remote_copy(
            src_ref=source,
            dst_ref=target,
            send_sem=send_sem.at[which],
            recv_sem=recv_sem.at[which],
            device_id=device,
            device_id_type=MESH,
        )
        for which, (source, target, device) in enumerate(plan)
    ]
    beside, upward, downward = copies[0:2], copies[2:7], copies[7:12]

    def each(items, act):
        for item in items:
            act(item)

    start, wait_recv, wait_send = (lambda c: c.start()), (lambda c: c.wait_recv()), (lambda c: c.wait_send())
    pl.when(north_here)(lambda: each(upward[3:], start))
    pl.when(south_here)(lambda: each(downward[3:], start))
    each(beside, start)
    pl.when(north_here)(lambda: each(upward[:3], start))
    pl.when(south_here)(lambda: each(downward[:3], start))
    if rounds:
        tell(0)

    thick.wait()
    depth = col_in[...].astype(jnp.float32)
    faces[0] = jnp.minimum(depth, roll(depth, -1, 1))
    faces[1] = jnp.minimum(depth, roll(depth, -1, 0))
    own_sum[...] = jnp.zeros((rows, cols), jnp.float32)

    def level(k, carry):
        below = lax.convert_element_type(k, jnp.float32)
        current = transport(fields[0, k], fields[1, k], fields[2, k], faces[0] > below, faces[1] > below)
        tracer_out[k] = current
        own_sum[...] += jnp.where(col_in[...] > k, thickness[k] * current, 0.0)
        return carry

    lax.fori_loop(0, levels, level, 0, unroll=2)

    def blank(rows_ref, halo):
        rows_ref[...] = jnp.zeros(rows_ref.shape, jnp.float32)
        flat[:, body, halo] = jnp.zeros((3, side_block, SUB, LANE), jnp.float32)
        own_tile[:, halo] = jnp.zeros((4, SUB, LANE), jnp.float32)
        for ref in (west, east):
            ref[halo] = jnp.zeros((SUB, LANE), jnp.float32)

    pl.when(jnp.logical_not(south_here))(lambda: blank(rows_south, low_halo))
    pl.when(jnp.logical_not(north_here))(lambda: blank(rows_north, high_halo))

    for turn in range(1, len(rounds)):
        hear(turn - 1)
        tell(turn)
    pl.when(south_here)(lambda: each(upward[:3], wait_recv))
    pl.when(north_here)(lambda: each(downward[:3], wait_recv))

    stacked_level = (iota((2 * SUB * levels, cols), 0) // (2 * SUB)).astype(jnp.float32)

    def row_strip(pieces, depth16, out):
        c, e, n = (jnp.concatenate(p, axis=0) for p in pieces)
        deep = jnp.concatenate([depth16] * levels, axis=0)
        open_east = jnp.minimum(deep, roll(deep, -1, 1)) > stacked_level
        open_nort = jnp.minimum(deep, roll(deep, -1, 0)) > stacked_level
        new = transport(c, e, n, open_east, open_nort)
        out[...] = new
        total = None
        for k in range(levels):
            term = jnp.where(depth16 > k, thickness[k] * new[2 * SUB * k : 2 * SUB * (k + 1)], 0.0)
            total = term if total is None else total + term
        return total

    south, north = ([], [], []), ([], [], [])
    for k in range(levels):
        a, b = rows_south[k, 0:SUB], rows_south[k, SUB : 2 * SUB]
        for f, halo in enumerate((a, b, jnp.where(sub < 6, roll(a, 3, 0), roll(b, -2, 0)))):
            south[f].extend([halo, fields[f, k, 0:SUB]])
        a, b = rows_north[k, 0:SUB], rows_north[k, SUB : 2 * SUB]
        for f, halo in enumerate((a, b, jnp.where(sub < 3, roll(a, -5, 0), roll(b, -1, 0)))):
            north[f].extend([fields[f, k, rows - SUB : rows], halo])
    def depth_rows(at):
        return jnp.concatenate([flat[0, b, at : at + 2 * SUB] for b in blocks], axis=1)

    sum_south = row_strip(south, depth_rows(0), strip_south)
    sum_north = row_strip(north, depth_rows(rows), strip_north)
    for b in blocks:
        here = slice(LANE * b, LANE * (b + 1))
        level_sum[b, 0:SUB] = sum_south[0:SUB, here]
        level_sum[b, inside] = own_sum[:, here]
        level_sum[b, SUB : SUB + 2] = sum_south[SUB : SUB + 2, here]
        level_sum[b, rows + SUB - 2 : rows + SUB] = sum_north[SUB - 2 : SUB, here]
        level_sum[b, rows + SUB : rows + 2 * SUB] = sum_north[SUB:, here]
        scale[b, 0 : rows + 2 * SUB] = 1.0 / (6.0 + flat[1, b])

    lane = iota((SUB, LANE), 1)
    group = lane // SEAM
    seat = lane % SEAM
    strip_level = group.astype(jnp.float32)
    lane_thickness = jnp.zeros((SUB, LANE), jnp.float32)
    for k in range(levels):
        lane_thickness = jnp.where(group == k, thickness[k], lane_thickness)
    low_half = lane < LANE // 2

    def side_lanes(base_west, base_east):
        return spare_lane(jnp.where(low_half, base_east + (lane & 3), base_west + ((lane - (LANE - 3)) & 3)))

    side_pick = [side_lanes(*bases) for bases in ((2, 0), (6, 6), (10, 10))]
    sides = []
    for got, shifts, first, in_halo in (
        (west, (3, -2, -6), 3, seat < SUB),
        (east, (8, 3, -2), 8, seat >= SUB),
    ):
        depth_pick = spare_lane(jnp.minimum(jnp.maximum(seat - first, 0), 4))
        sides.append((got, shifts, depth_pick, in_halo))

    each(beside, wait_recv)
    pl.when(south_here)(lambda: each(upward[3:], wait_recv))
    pl.when(north_here)(lambda: each(downward[3:], wait_recv))

    def at(start):
        return slice(start, start + SUB)

    for r in range(0, rows + 2 * SUB, SUB):
        for w, (got, shifts, depth_pick, in_halo) in enumerate(sides):
            sent = got[at(r)]
            moved = [roll(sent, shift, 1) for shift in shifts] + [pick(sent, depth_pick)]
            for f in range(4):
                strips[w, f, at(r)] = jnp.where(in_halo, moved[f], own_tile[f, at(r)])
    for r in range(0, rows + 2 * SUB, SUB):
        for w in range(2):
            deep = strips[w, 3, at(r)]
            open_east = jnp.minimum(deep, roll(deep, -1, 1)) > strip_level
            open_nort = jnp.minimum(deep, strips[w, 3, at(r + 1)]) > strip_level
            strips[w, 1, at(r)] = jnp.where(open_east, strips[w, 1, at(r)], 0.0)
            strips[w, 2, at(r)] = jnp.where(open_nort, strips[w, 2, at(r)], 0.0)

    def side_step(w, f, r):
        here, ahead, behind = (strips[w, f, at(r + d)] for d in (0, 1, -1))
        fast_east, fast_north, fast_south = strips[w, 1, at(r)], strips[w, 2, at(r)], strips[w, 2, at(r - 1)]
        flux_east = fast_east * jnp.where(fast_east > 0.0, here, roll(here, -1, 1))
        flux_north = fast_north * jnp.where(fast_north > 0.0, here, ahead)
        flux_south = fast_south * jnp.where(fast_south > 0.0, behind, here)
        return here - (flux_east - roll(flux_east, 1, 1) + flux_north - flux_south)

    for r in range(SUB - 4, rows + SUB + 4, SUB):
        for w in range(2):
            strips[w, 4, at(r)] = side_step(w, 0, r)
    inner_rows = range(SUB - 3, rows + SUB + 3, SUB)
    for r in inner_rows:
        for w in range(2):
            new = side_step(w, 4, r)
            strips[w, 5, at(r)] = new
            strips[w, 0, at(r)] = jnp.where(strips[w, 3, at(r)] > strip_level, lane_thickness * new, 0.0)
    for f, lanes in enumerate(side_pick):
        for r in range(0, rows + 2 * SUB, SUB):
            flat[f, side_block, at(r)] = jnp.where(low_half, pick(east[at(r)], lanes), pick(west[at(r)], lanes))
    for r in inner_rows:
        for w in range(2):
            total = strips[w, 0, at(r)]
            strips[w, 1, at(r)] = total + roll(total, LANE // 2, 1)
    for r in inner_rows:
        for w in range(2):
            total = strips[w, 1, at(r)]
            strips[w, 2, at(r)] = sum(roll(total, shift - SUB, 1) for shift in range(0, LANE // 2, SEAM))
    for r in inner_rows:
        sum_west, sum_east = strips[0, 2, at(r)], strips[1, 2, at(r)]
        for b in range(side_block + 1):
            if b < side_block:
                total, inverse = level_sum[b, at(r)], scale[b, at(r)]
                if b == 0:
                    total = jnp.where(lane < 2, sum_west, total)
                if b == side_block - 1:
                    total = jnp.where(lane >= LANE - 2, sum_east, total)
            else:
                total = jnp.where(low_half, sum_east, sum_west)
                inverse = 1.0 / (6.0 + flat[1, b, at(r)])
            z0 = (flat[2, b, at(r)] + total) * inverse
            if b < side_block:
                level_sum[b, at(r)] = z0
            wet = flat[0, b, at(r)] > 0.0
            scale[b, at(r)] = jnp.where(wet, inverse, 0.0)
            start_vec[0, b, at(r)] = jnp.where(wet, z0, 0.0)

    def off_diagonal(source, r, wanted):
        upright, mixed = [], []
        for b in range(side_block + 1):
            both = start_vec[source, b, at(r - 1)] + start_vec[source, b, at(r + 1)]
            upright.append(both)
            mixed.append(start_vec[source, b, at(r)] + 0.5 * both)
        ahead, behind = ([roll(m, d, 1) for m in mixed] for d in (-1, 1))
        out = []
        for b in range(wanted):
            after = jnp.where(lane < LANE - 1, ahead[b], ahead[(b + 1) % (side_block + 1)])
            before = jnp.where(lane > 0, behind[b], behind[b - 1])
            out.append(scale[b, at(r)] * (upright[b] + after + before))
        return out

    for power in (1, 2):
        for r in range(SUB - 3 + power, rows + SUB + 3 - power, SUB):
            for b, z in enumerate(off_diagonal(power - 1, r, side_block + 1)):
                start_vec[power, b, at(r)] = z

    sums = [jnp.zeros((SUB, LANE), jnp.float32)] * (2 * ITERS)
    for r in range(SUB, rows + SUB, SUB):
        for b, z3 in enumerate(off_diagonal(2, r, side_block)):
            z = [level_sum[b, at(r)], start_vec[1, b, at(r)], start_vec[2, b, at(r)], z3]
            for i in range(ITERS):
                basis_out[i, b, at(r - SUB)] = z[i]
                scaled = (6.0 + flat[1, b, at(r)]) * z[i]
                sums[2 * i] += scaled * z[i]
                sums[2 * i + 1] += scaled * z[i + 1]
    sums = [jnp.sum(total, axis=0, keepdims=True) for total in sums]
    folded = jnp.concatenate(sums + [jnp.zeros((SUB - len(sums), LANE), jnp.float32)], axis=0)
    diag = iota((SUB, LANE), 1) == iota((SUB, LANE), 0)
    folded = jnp.sum(folded, axis=1, keepdims=True)
    part[...] = jnp.sum(jnp.where(diag, folded, 0.0), axis=0, keepdims=True)

    if rounds:
        hear(len(rounds) - 1)
    for index, target in enumerate(others):
        pltpu.make_async_remote_copy(
            src_ref=part,
            dst_ref=slots.at[index],
            send_sem=sum_send_sem,
            recv_sem=sum_recv_sem,
            device_id=target,
            device_id_type=MESH,
        ).start()

    for k in range(levels):
        tracer_out[k, 0:SUB] = jnp.where(sub < 2, strip_south[2 * SUB * k + SUB : 2 * SUB * (k + 1)], tracer_out[k, 0:SUB])
        tracer_out[k, rows - SUB : rows] = jnp.where(
            sub >= SUB - 2, strip_north[2 * SUB * k : 2 * SUB * k + SUB], tracer_out[k, rows - SUB : rows]
        )
    lane = iota((rows, LANE), 1)
    side_new = jnp.where(lane % SEAM < SUB, strips[1, 5, inside], strips[0, 5, inside])
    for k in range(levels):
        moved = roll(side_new, -SEAM * k - SUB, 1)
        tracer_out[k, :, 0:LANE] = jnp.where(lane < 2, moved, tracer_out[k, :, 0:LANE])
        tracer_out[k, :, cols - LANE : cols] = jnp.where(lane >= LANE - 2, moved, tracer_out[k, :, cols - LANE : cols])

    everything = pltpu.make_async_remote_copy(
        src_ref=slots,
        dst_ref=slots,
        send_sem=sum_send_sem,
        recv_sem=sum_recv_sem,
        device_id=others[0],
        device_id_type=MESH,
    )
    everything.wait_recv()
    moments_out[...] = jnp.sum(slots[...], axis=0) + part[...]

    everything.wait_send()
    each(beside, wait_send)
    pl.when(north_here)(lambda: each(upward, wait_send))
    pl.when(south_here)(lambda: each(downward, wait_send))


def finish(tracer_ref, basis_ref, moments_ref, tracer_out, heights_out, heights, save):
    levels = tracer_ref.shape[0]
    saves = [pltpu.make_async_copy(tracer_ref.at[k], tracer_out.at[k], save.at[k]) for k in range(levels)]
    for copy in saves:
        copy.start()
    diag = iota((SUB, LANE), 1) == iota((SUB, LANE), 0)
    total = jnp.broadcast_to(moments_ref[...], (SUB, LANE))
    total = jnp.sum(jnp.where(diag, total, 0.0), axis=1, keepdims=True)
    moment = [total[i : i + 1, :] for i in range(2 * ITERS)]

    def inner(a, b):
        return sum(x * y * moment[i + j] for i, x in enumerate(a) for j, y in enumerate(b))

    def ratio(top, bottom):
        good = bottom > 0.0
        return jnp.where(good, top / jnp.where(good, bottom, 1.0), 0.0)

    one, zero = jnp.ones((1, 1), jnp.float32), jnp.zeros((1, 1), jnp.float32)
    scaled, direction, height = [one], [one], [zero] * ITERS
    product_now = moment[0]
    for iteration in range(ITERS):
        low, high = direction + [zero], [zero] + direction
        applied = [a - b for a, b in zip(low, high)]
        step_size = ratio(product_now, inner(direction, applied))
        for i, x in enumerate(direction):
            height[i] = height[i] + step_size * x
        if iteration + 1 < ITERS:
            scaled = [a - step_size * b for a, b in zip(scaled + [zero], applied)]
            product_next = jnp.maximum(inner(scaled, scaled), 0.0)
            factor = ratio(product_next, product_now)
            direction = [a + factor * b for a, b in zip(scaled, low)]
            product_now = product_next
    for b in range(basis_ref.shape[1]):
        heights[:, LANE * b : LANE * (b + 1)] = sum(h * basis_ref[i, b] for i, h in enumerate(height))

    saves.append(pltpu.make_async_copy(heights, heights_out, save.at[levels]))
    saves[-1].start()
    for copy in saves:
        copy.wait()


def on_device(ny, nx, tracer, east_speed, north_speed, columns, thickness, surface_flux, helm):
    levels, rows, cols = tracer.shape
    hbm = pl.BlockSpec(memory_space=pl.ANY)
    vmem = pl.BlockSpec(memory_space=pltpu.VMEM)
    f32 = jnp.float32
    dma = pltpu.SemaphoreType.DMA
    blocks = cols // LANE
    tall = rows + 2 * SUB
    scratch = [
        pltpu.VMEM((3, levels, rows, cols), f32),
        pltpu.VMEM((rows, cols), jnp.int32),
        pltpu.VMEM((3, blocks + 1, tall, LANE), f32),
        pltpu.VMEM((4, tall, LANE), f32),
        *[pltpu.VMEM((rows, LANE), f32)] * 2,
        *[pltpu.VMEM((tall, LANE), f32)] * 2,
        *[pltpu.VMEM((levels, 2 * SUB, cols), f32)] * 4,
        *[pltpu.VMEM((levels * 2 * SUB, cols), f32)] * 2,
        pltpu.VMEM((rows, cols), f32),
        pltpu.VMEM((2, rows, cols), f32),
        pltpu.VMEM((2, 6, tall + SUB, LANE), f32),
        pltpu.VMEM((blocks + 1, tall, LANE), f32),
        pltpu.VMEM((blocks + 1, tall, LANE), f32),
        pltpu.VMEM((ITERS, blocks + 1, tall + SUB, LANE), f32),
        pltpu.VMEM((1, LANE), f32),
        pltpu.VMEM((ny * nx - 1, 1, LANE), f32),
        pltpu.SMEM((levels,), f32),
        pltpu.SemaphoreType.REGULAR((max(ny, nx).bit_length(),)),
        dma((7 + 2 * blocks,)),
        dma((12,)),
        dma((12,)),
        dma,
        dma,
    ]
    results = pl.pallas_call(
        functools.partial(kernel, ny, nx),
        out_shape=(
            pltpu.VMEM((levels, rows, cols), f32),
            pltpu.VMEM((ITERS, blocks, rows, LANE), f32),
            pltpu.VMEM((1, LANE), f32),
        ),
        in_specs=[hbm] * 7,
        out_specs=(vmem,) * 3,
        scratch_shapes=scratch,
        compiler_params=pltpu.CompilerParams(collective_id=0, has_side_effects=True),
    )(tracer, east_speed, north_speed, columns, thickness, surface_flux, helm)
    return pl.pallas_call(
        finish,
        out_shape=(
            jax.ShapeDtypeStruct((levels, rows, cols), f32),
            jax.ShapeDtypeStruct((rows, cols), f32),
        ),
        in_specs=[vmem] * 3,
        out_specs=(hbm, hbm),
        scratch_shapes=[pltpu.VMEM((rows, cols), f32), dma((levels + 1,))],
    )(*[pltpu.with_memory_space_constraint(r, pltpu.VMEM) for r in results])


def solution(mesh):
    spec = P(None, "gy", "gx")
    flat = P("gy", "gx")
    return jax.shard_map(
        functools.partial(on_device, mesh.shape["gy"], mesh.shape["gx"]),
        mesh=mesh,
        in_specs=(spec, spec, spec, flat, P(), flat, flat),
        out_specs=(spec, flat),
        check_vma=False,
    )
```

time: 20.8 us -> 20.3 us (0.976)
  Pallas kernels: 20 us -> 19.5 us
    pallas_call x1, Pallas kernels: 18.9 us -> 18.4 us  [on_device(): pl.pallas_call(functools.partial(kernel, ny, nx), out_shape=(pltpu.VMEM((...]
where the time goes in v2:
time: 20.3 us; the launch traced here: 20.1 us
  Pallas kernels  19.5 us (96%)
  between operations  0.64 us (3%)
    pallas_call x1, Pallas kernels, on_device(): pl.pallas_call(functools.partial(kernel, ny, nx), out_shape=(pltpu.VMEM((...  18.4 us
    pallas_call x1, Pallas kernels, on_device(): pl.pallas_call(finish, out_shape=(jax.ShapeDtypeStruct((levels, rows, col...  1.08 us

profile of v2, /device:TPU:0, one launch (start us, length us, event | category | flops | bytes accessed | tf_op | source)
XLA Modules:
  0.0 20.1 jit_solution(519780939443627432)
XLA Ops:
  0.6 18.4 %shard_map.86 = (f32[8,128,256]{2,1,0:T(8,128)S(1)}, f32[3,2,128,128]{3,2,1,0:T(8,128)S(1)}, f32[1,128]{1,0:T(1,128)S(1)}) custom-call(f32[8,128,256]{2,1,0:T(8,128)} %tracer_ref.1, f32[8,128,256]{2,1,0:T(8,128)} %east_ref.1, f32[8,128,256]{2,1,0:T(8,128)} %north_ref.1, s32[128,256]{1,0:T(8,128)} %columns_ref.1, f32[8]{0:T(128)} %thick_hbm.1, ...), custom_call_target="tpu_custom_call" | custom-call | tf_op jit(solution)/shard_map/pallas_call | solution.py:540
  19.0 1.1 %shard_map.87 = (f32[8,128,256]{2,1,0:T(8,128)}, f32[128,256]{1,0:T(8,128)}) custom-call(f32[8,128,256]{2,1,0:T(8,128)S(1)} %get-tuple-element.5.tracer_ref, f32[3,2,128,128]{3,2,1,0:T(8,128)S(1)} %get-tuple-element.6.basis_ref, f32[1,128]{1,0:T(1,128)S(1)} %get-tuple-element.7.moments_ref), custom_call_target="tpu_custom_call" | custom-call | tf_op jit(solution)/shard_map/pallas_call | solution.py:552

commit v3 on v2

--- a/solution.py
+++ b/solution.py
@@ -63,8 +63,7 @@
     rows_down,
     rows_south,
     rows_north,
-    strip_south,
-    strip_north,
+    row_strips,
     own_sum,
     faces,
     strips,
@@ -178,30 +177,38 @@
     to_east[...] = message((-3, 2, 6), spare_east)
     to_west[...] = message((-8, -3, 2), spare_west)
 
-    sub = iota((SUB, cols), 0)
+    sub = iota((SUB, LANE), 0)
+    spare_up = ((0, -1), (0, -3), (0, -5), (1, -3), (1, -5), (2, -3), (2, -5))
+    spare_down = ((0, 5), (0, 2), (1, 5), (2, 5))
+
+    def spare_rows(which, k, b, where):
+        field, turn = which[min(k, len(which) - 1)]
+        return roll(flat[field, b, where], turn, 0)
+
     for k in range(levels):
-        c, e, n = (fields[f, k, rows - SUB : rows] for f in range(3))
-        rows_up[k, 0:SUB] = jnp.where(sub < 3, roll(n, -3, 0), c)
-        rows_up[k, SUB : 2 * SUB] = jnp.where(sub < 4, roll(n, 2, 0), e)
-        c, e, n = (fields[f, k, 0:SUB] for f in range(3))
-        rows_down[k, 0:SUB] = jnp.where(sub < 5, c, roll(n, 5, 0))
-        rows_down[k, SUB : 2 * SUB] = jnp.where(sub < 4, e, roll(n, 1, 0))
+        for b in blocks:
+            here = slice(LANE * b, LANE * (b + 1))
+            c, e, n = (fields[f, k, rows - SUB : rows, here] for f in range(3))
+            rows_up[k, b, 0:SUB] = jnp.where(sub < 3, roll(n, -3, 0), c)
+            rows_up[k, b, SUB : 2 * SUB] = jnp.where(
+                sub < 2, roll(n, 2, 0), jnp.where(sub < 4, spare_rows(spare_up, k, b, high_own), e)
+            )
+            c, e, n = (fields[f, k, 0:SUB, here] for f in range(3))
+            rows_down[k, b, 0:SUB] = jnp.where(sub < 5, c, roll(n, 5, 0))
+            rows_down[k, b, SUB : 2 * SUB] = jnp.where(
+                sub < 4, e, jnp.where(sub < 5, roll(n, 1, 0), spare_rows(spare_down, k, b, low_own))
+            )
 
     pl.semaphore_wait(barrier, len(greeted))
 
     up, down, right, left = wrap(my_y + 1, ny), wrap(my_y + ny - 1, ny), xs[1], xs[-1]
-    body = pl.ds(0, side_block)
     plan = [
         (to_east, west.at[inside], (my_y, right)),
         (to_west, east.at[inside], (my_y, left)),
         (rows_up, rows_south, (up, my_x)),
-        (flat.at[:, body, high_own], flat.at[:, body, low_halo], (up, my_x)),
-        (own_tile.at[:, high_own], own_tile.at[:, low_halo], (up, my_x)),
         (to_east.at[last_rows], west.at[low_halo], (up, right)),
         (to_west.at[last_rows], east.at[low_halo], (up, left)),
         (rows_down, rows_north, (down, my_x)),
-        (flat.at[:, body, low_own], flat.at[:, body, high_halo], (down, my_x)),
-        (own_tile.at[:, low_own], own_tile.at[:, high_halo], (down, my_x)),
         (to_east.at[first_rows], west.at[high_halo], (down, right)),
         (to_west.at[first_rows], east.at[high_halo], (down, left)),
     ]
@@ -216,18 +223,18 @@
         )
         for which, (source, target, device) in enumerate(plan)
     ]
-    beside, upward, downward = copies[0:2], copies[2:7], copies[7:12]
+    beside, upward, downward = copies[0:2], copies[2:5], copies[5:8]
 
     def each(items, act):
         for item in items:
             act(item)
 
     start, wait_recv, wait_send = (lambda c: c.start()), (lambda c: c.wait_recv()), (lambda c: c.wait_send())
-    pl.when(north_here)(lambda: each(upward[3:], start))
-    pl.when(south_here)(lambda: each(downward[3:], start))
+    pl.when(north_here)(lambda: each(upward[1:], start))
+    pl.when(south_here)(lambda: each(downward[1:], start))
     each(beside, start)
-    pl.when(north_here)(lambda: each(upward[:3], start))
-    pl.when(south_here)(lambda: each(downward[:3], start))
+    pl.when(north_here)(lambda: each(upward[:1], start))
+    pl.when(south_here)(lambda: each(downward[:1], start))
     if rounds:
         tell(0)
 
@@ -248,8 +255,6 @@
 
     def blank(rows_ref, halo):
         rows_ref[...] = jnp.zeros(rows_ref.shape, jnp.float32)
-        flat[:, body, halo] = jnp.zeros((3, side_block, SUB, LANE), jnp.float32)
-        own_tile[:, halo] = jnp.zeros((4, SUB, LANE), jnp.float32)
         for ref in (west, east):
             ref[halo] = jnp.zeros((SUB, LANE), jnp.float32)
 
@@ -259,55 +264,106 @@
     for turn in range(1, len(rounds)):
         hear(turn - 1)
         tell(turn)
-    pl.when(south_here)(lambda: each(upward[:3], wait_recv))
-    pl.when(north_here)(lambda: each(downward[:3], wait_recv))
-
-    stacked_level = (iota((2 * SUB * levels, cols), 0) // (2 * SUB)).astype(jnp.float32)
-
-    def row_strip(pieces, depth16, out):
-        c, e, n = (jnp.concatenate(p, axis=0) for p in pieces)
-        deep = jnp.concatenate([depth16] * levels, axis=0)
-        open_east = jnp.minimum(deep, roll(deep, -1, 1)) > stacked_level
-        open_nort = jnp.minimum(deep, roll(deep, -1, 0)) > stacked_level
-        new = transport(c, e, n, open_east, open_nort)
-        out[...] = new
-        total = None
-        for k in range(levels):
-            term = jnp.where(depth16 > k, thickness[k] * new[2 * SUB * k : 2 * SUB * (k + 1)], 0.0)
-            total = term if total is None else total + term
-        return total
-
-    south, north = ([], [], []), ([], [], [])
-    for k in range(levels):
-        a, b = rows_south[k, 0:SUB], rows_south[k, SUB : 2 * SUB]
-        for f, halo in enumerate((a, b, jnp.where(sub < 6, roll(a, 3, 0), roll(b, -2, 0)))):
-            south[f].extend([halo, fields[f, k, 0:SUB]])
-        a, b = rows_north[k, 0:SUB], rows_north[k, SUB : 2 * SUB]
-        for f, halo in enumerate((a, b, jnp.where(sub < 3, roll(a, -5, 0), roll(b, -1, 0)))):
-            north[f].extend([fields[f, k, rows - SUB : rows], halo])
-    def depth_rows(at):
-        return jnp.concatenate([flat[0, b, at : at + 2 * SUB] for b in blocks], axis=1)
-
-    sum_south = row_strip(south, depth_rows(0), strip_south)
-    sum_north = row_strip(north, depth_rows(rows), strip_north)
-    for b in blocks:
-        here = slice(LANE * b, LANE * (b + 1))
-        level_sum[b, 0:SUB] = sum_south[0:SUB, here]
-        level_sum[b, inside] = own_sum[:, here]
-        level_sum[b, SUB : SUB + 2] = sum_south[SUB : SUB + 2, here]
-        level_sum[b, rows + SUB - 2 : rows + SUB] = sum_north[SUB - 2 : SUB, here]
-        level_sum[b, rows + SUB : rows + 2 * SUB] = sum_north[SUB:, here]
-        scale[b, 0 : rows + 2 * SUB] = 1.0 / (6.0 + flat[1, b])
+    pl.when(south_here)(lambda: each(upward[:1], wait_recv))
+    pl.when(north_here)(lambda: each(downward[:1], wait_recv))
+
+    def at(start):
+        return slice(start, start + SUB)
 
     lane = iota((SUB, LANE), 1)
     group = lane // SEAM
     seat = lane % SEAM
+    low_half = lane < LANE // 2
+
+    def beyond(values, step):
+        turned = [roll(v, -step, 1) for v in values]
+        near = lane < LANE - 1 if step > 0 else lane > 0
+        return [jnp.where(near, t, turned[(b + step) % len(values)]) for b, t in enumerate(turned)]
+
+    def receive_south(k):
+        for b in blocks:
+            first, second = rows_south[k, b, 0:SUB], rows_south[k, b, SUB : 2 * SUB]
+            yield first, second, jnp.where(sub < 6, roll(first, 3, 0), roll(second, -2, 0))
+
+    def receive_north(k):
+        for b in blocks:
+            first, second = rows_north[k, b, 0:SUB], rows_north[k, b, SUB : 2 * SUB]
+            yield first, second, jnp.where(sub < 3, roll(first, -5, 0), roll(second, -1, 0))
+
+    for b in blocks:
+        spare = [rows_south[k, b, SUB : 2 * SUB] for k in range(7)]
+        flat[0, b, low_halo] = jnp.where(
+            sub < 5, roll(spare[0], 1, 0), jnp.where(sub < 7, roll(spare[1], 3, 0), roll(spare[2], 5, 0))
+        )
+        for f in (1, 2):
+            flat[f, b, low_halo] = jnp.where(sub < 7, roll(spare[2 * f + 1], 3, 0), roll(spare[2 * f + 2], 5, 0))
+        spare = [rows_north[k, b, SUB : 2 * SUB] for k in range(4)]
+        flat[0, b, high_halo] = jnp.where(sub < 3, roll(spare[0], -5, 0), roll(spare[1], -2, 0))
+        for f in (1, 2):
+            flat[f, b, high_halo] = roll(spare[f + 1], -5, 0)
+        scale[b] = 1.0 / (6.0 + flat[1, b, 0 : rows + 2 * SUB])
+    depth_lanes = (LANE - SUB + seat) % LANE
+    for halo in (low_halo, high_halo):
+        own_tile[3, halo] = pick(jnp.where(low_half, flat[0, 0, halo], flat[0, side_block - 1, halo]), depth_lanes)
+
+    row_sides = ((0, receive_south, 0, SUB, 0, low_halo), (1, receive_north, SUB, 0, rows, high_halo))
+    for w, receive, halo_at, own_at, base, halo in row_sides:
+        open_east, open_nort = [], []
+        for r in (0, SUB):
+            deep = [flat[0, b, at(base + r)] for b in blocks]
+            open_east.append([jnp.minimum(d, e) for d, e in zip(deep, beyond(deep, 1))])
+            ahead = [flat[0, b, at(base + r + 1)] for b in blocks]
+            open_nort.append([jnp.minimum(d, a) for d, a in zip(deep, ahead)])
+        packed = [None] * 3
+        own_rows = pl.ds(0, SUB) if w == 0 else pl.ds(rows - SUB, SUB)
+        for k in range(levels):
+            got = list(receive(k))
+            for f in range(3):
+                moved = roll(jnp.where(low_half, got[0][f], got[-1][f]), SEAM * k + SUB, 1)
+                packed[f] = moved if packed[f] is None else jnp.where(group == k, moved, packed[f])
+            for b in blocks:
+                for r, values in (
+                    (halo_at, got[b]),
+                    (own_at, [fields[f, k, own_rows, LANE * b : LANE * (b + 1)] for f in range(3)]),
+                ):
+                    t = r // SUB
+                    row_strips[w, 0, k, b, at(r)] = values[0]
+                    row_strips[w, 1, k, b, at(r)] = jnp.where(open_east[t][b] > k, values[1], 0.0)
+                    row_strips[w, 2, k, b, at(r)] = jnp.where(open_nort[t][b] > k, values[2], 0.0)
+        for f in range(3):
+            own_tile[f, halo] = packed[f]
+
+    def row_step(w, f, k, r):
+        here, ahead, behind = ([row_strips[w, f, k, b, at(r + d)] for b in blocks] for d in (0, 1, -1))
+        fast_east, fast_north = ([row_strips[w, g, k, b, at(r)] for b in blocks] for g in (1, 2))
+        fast_south = [row_strips[w, 2, k, b, at(r - 1)] for b in blocks]
+        flux_east = [v * jnp.where(v > 0.0, c, x) for v, c, x in zip(fast_east, here, beyond(here, 1))]
+        out = []
+        for b, flux_west in enumerate(beyond(flux_east, -1)):
+            flux_north = fast_north[b] * jnp.where(fast_north[b] > 0.0, here[b], ahead[b])
+            flux_south = fast_south[b] * jnp.where(fast_south[b] > 0.0, behind[b], here[b])
+            out.append(here[b] - (flux_east[b] - flux_west + flux_north - flux_south))
+        return out
+
+    for k in range(levels):
+        for w in range(2):
+            for b, new in enumerate(row_step(w, 0, k, SUB - 4)):
+                row_strips[w, 3, k, b, at(SUB - 4)] = new
+    row_sums = [[jnp.zeros((SUB, LANE), jnp.float32) for _ in blocks] for _ in range(2)]
+    for k in range(levels):
+        for w, base in enumerate((0, rows)):
+            for b, new in enumerate(row_step(w, 3, k, SUB - 3)):
+                row_strips[w, 4, k, b, at(SUB - 3)] = new
+                row_sums[w][b] += jnp.where(flat[0, b, at(base + SUB - 3)] > k, thickness[k] * new, 0.0)
+    for b in blocks:
+        level_sum[b, inside] = own_sum[:, LANE * b : LANE * (b + 1)]
+        level_sum[b, SUB - 3 : SUB + 2] = row_sums[0][b][0:5]
+        level_sum[b, rows + SUB - 2 : rows + SUB + 3] = row_sums[1][b][1:6]
+
     strip_level = group.astype(jnp.float32)
     lane_thickness = jnp.zeros((SUB, LANE), jnp.float32)
     for k in range(levels):
         lane_thickness = jnp.where(group == k, thickness[k], lane_thickness)
-    low_half = lane < LANE // 2
-
     def side_lanes(base_west, base_east):
         return spare_lane(jnp.where(low_half, base_east + (lane & 3), base_west + ((lane - (LANE - 3)) & 3)))
 
@@ -321,11 +377,8 @@
         sides.append((got, shifts, depth_pick, in_halo))
 
     each(beside, wait_recv)
-    pl.when(south_here)(lambda: each(upward[3:], wait_recv))
-    pl.when(north_here)(lambda: each(downward[3:], wait_recv))
-
-    def at(start):
-        return slice(start, start + SUB)
+    pl.when(south_here)(lambda: each(upward[1:], wait_recv))
+    pl.when(north_here)(lambda: each(downward[1:], wait_recv))
 
     for r in range(0, rows + 2 * SUB, SUB):
         for w, (got, shifts, depth_pick, in_halo) in enumerate(sides):
@@ -435,10 +488,10 @@
         ).start()
 
     for k in range(levels):
-        tracer_out[k, 0:SUB] = jnp.where(sub < 2, strip_south[2 * SUB * k + SUB : 2 * SUB * (k + 1)], tracer_out[k, 0:SUB])
-        tracer_out[k, rows - SUB : rows] = jnp.where(
-            sub >= SUB - 2, strip_north[2 * SUB * k : 2 * SUB * k + SUB], tracer_out[k, rows - SUB : rows]
-        )
+        for b in blocks:
+            here = slice(LANE * b, LANE * (b + 1))
+            tracer_out[k, 0:2, here] = row_strips[0, 4, k, b, SUB : SUB + 2]
+            tracer_out[k, rows - 2 : rows, here] = row_strips[1, 4, k, b, SUB - 2 : SUB]
     lane = iota((rows, LANE), 1)
     side_new = jnp.where(lane % SEAM < SUB, strips[1, 5, inside], strips[0, 5, inside])
     for k in range(levels):
@@ -515,12 +568,12 @@
     scratch = [
         pltpu.VMEM((3, levels, rows, cols), f32),
         pltpu.VMEM((rows, cols), jnp.int32),
-        pltpu.VMEM((3, blocks + 1, tall, LANE), f32),
+        pltpu.VMEM((3, blocks + 1, tall + SUB, LANE), f32),
         pltpu.VMEM((4, tall, LANE), f32),
         *[pltpu.VMEM((rows, LANE), f32)] * 2,
         *[pltpu.VMEM((tall, LANE), f32)] * 2,
-        *[pltpu.VMEM((levels, 2 * SUB, cols), f32)] * 4,
-        *[pltpu.VMEM((levels * 2 * SUB, cols), f32)] * 2,
+        *[pltpu.VMEM((levels, blocks, 2 * SUB, LANE), f32)] * 4,
+        pltpu.VMEM((2, 5, levels, blocks, 2 * SUB, LANE), f32),
         pltpu.VMEM((rows, cols), f32),
         pltpu.VMEM((2, rows, cols), f32),
         pltpu.VMEM((2, 6, tall + SUB, LANE), f32),
@@ -532,8 +585,8 @@
         pltpu.SMEM((levels,), f32),
         pltpu.SemaphoreType.REGULAR((max(ny, nx).bit_length(),)),
         dma((7 + 2 * blocks,)),
-        dma((12,)),
-        dma((12,)),
+        dma((8,)),
+        dma((8,)),
         dma,
         dma,
     ]

time: 20.3 us -> 20.2 us (level)
  no operation moved by 1% of the time
where the time goes in v3:
time: 20.2 us; the launch traced here: 20 us
  Pallas kernels  19.4 us (96%)
  between operations  0.64 us (3%)
    pallas_call x1, Pallas kernels, on_device(): pl.pallas_call(functools.partial(kernel, ny, nx), out_shape=(pltpu.VMEM((...  18.3 us
    pallas_call x1, Pallas kernels, on_device(): pl.pallas_call(finish, out_shape=(jax.ShapeDtypeStruct((levels, rows, col...  1.08 us

profile of v3, /device:TPU:0, one launch (start us, length us, event | category | flops | bytes accessed | tf_op | source)
XLA Modules:
  0.0 20.0 jit_solution(3365618075349177789)
XLA Ops:
  0.6 18.3 %shard_map.86 = (f32[8,128,256]{2,1,0:T(8,128)S(1)}, f32[3,2,128,128]{3,2,1,0:T(8,128)S(1)}, f32[1,128]{1,0:T(1,128)S(1)}) custom-call(f32[8,128,256]{2,1,0:T(8,128)} %tracer_ref.1, f32[8,128,256]{2,1,0:T(8,128)} %east_ref.1, f32[8,128,256]{2,1,0:T(8,128)} %north_ref.1, s32[128,256]{1,0:T(8,128)} %columns_ref.1, f32[8]{0:T(128)} %thick_hbm.1, ...), custom_call_target="tpu_custom_call" | custom-call | tf_op jit(solution)/shard_map/pallas_call | solution.py:593
  19.0 1.1 %shard_map.87 = (f32[8,128,256]{2,1,0:T(8,128)}, f32[128,256]{1,0:T(8,128)}) custom-call(f32[8,128,256]{2,1,0:T(8,128)S(1)} %get-tuple-element.5.tracer_ref, f32[3,2,128,128]{3,2,1,0:T(8,128)S(1)} %get-tuple-element.6.basis_ref, f32[1,128]{1,0:T(1,128)S(1)} %get-tuple-element.7.moments_ref), custom_call_target="tpu_custom_call" | custom-call | tf_op jit(solution)/shard_map/pallas_call | solution.py:605

commit v4 on v3

--- a/solution.py
+++ b/solution.py
@@ -95,16 +95,24 @@
     side_block = cols // LANE
     inside = pl.ds(SUB, rows)
     small = [pltpu.make_async_copy(columns_ref, col_in, in_sem.at[0])] + [
-        pltpu.make_async_copy(ref.at[:, pl.ds(LANE * b, LANE)], flat.at[f, b, inside], in_sem.at[7 + len(blocks) * (f - 1) + b])
+        pltpu.make_async_copy(ref.at[:, pl.ds(LANE * b, LANE)], flat.at[f, b, inside], in_sem.at[1 + len(blocks) * (f - 1) + b])
         for f, ref in ((1, helm_ref), (2, surface_ref))
         for b in blocks
     ]
+    halves = [range(0, levels // 2), range(levels // 2, levels)]
     large = [
-        pltpu.make_async_copy(ref, fields.at[f], in_sem.at[3 + f])
+        [
+            pltpu.make_async_copy(
+                ref.at[pl.ds(half[0], len(half))],
+                fields.at[f, pl.ds(half[0], len(half))],
+                in_sem.at[1 + 2 * len(blocks) + 2 * f + h],
+            )
+            for h, half in enumerate(halves)
+        ]
         for f, ref in enumerate((tracer_ref, east_ref, north_ref))
     ]
-    thick = pltpu.make_async_copy(thick_hbm, thickness, in_sem.at[6])
-    for load in small + large + [thick]:
+    thick = pltpu.make_async_copy(thick_hbm, thickness, in_sem.at[7 + 2 * len(blocks)])
+    for load in small + sum(large, []) + [thick]:
         load.start()
     barrier = pltpu.get_barrier_semaphore()
 
@@ -160,23 +168,6 @@
     east_from = jnp.where(slot < 6, LANE - 5 + slot, jnp.where(slot < 10, slot - 6 + 13, slot - 10 + 29)) % LANE
     west_from = jnp.where(slot < 6, slot, jnp.where(slot < 10, slot - 6 + 16, slot - 10 + 32)) % LANE
     spare_east, spare_west = pick(three, east_from), pick(three, west_from)
-    tiles = []
-    for f in range(3):
-        large[f].wait()
-        packed = None
-        for k in range(levels):
-            moved = roll(both_edges(fields[f, k, :, 0:LANE], fields[f, k, :, cols - LANE : cols]), SEAM * k + SUB, 1)
-            packed = moved if packed is None else jnp.where(group == k, moved, packed)
-        own_tile[f, inside] = packed
-        tiles.append(packed)
-
-    def message(shifts, spare):
-        c, e, n = (roll(tile, shift, 1) for tile, shift in zip(tiles, shifts))
-        return jnp.where(seat < 5, c, jnp.where(seat < 10, e, jnp.where(seat < SEAM - 2, n, spare)))
-
-    to_east[...] = message((-3, 2, 6), spare_east)
-    to_west[...] = message((-8, -3, 2), spare_west)
-
     sub = iota((SUB, LANE), 0)
     spare_up = ((0, -1), (0, -3), (0, -5), (1, -3), (1, -5), (2, -3), (2, -5))
     spare_down = ((0, 5), (0, 2), (1, 5), (2, 5))
@@ -185,7 +176,7 @@
         field, turn = which[min(k, len(which) - 1)]
         return roll(flat[field, b, where], turn, 0)
 
-    for k in range(levels):
+    def pack_rows(k):
         for b in blocks:
             here = slice(LANE * b, LANE * (b + 1))
             c, e, n = (fields[f, k, rows - SUB : rows, here] for f in range(3))
@@ -198,6 +189,23 @@
             rows_down[k, b, SUB : 2 * SUB] = jnp.where(
                 sub < 4, e, jnp.where(sub < 5, roll(n, 1, 0), spare_rows(spare_down, k, b, low_own))
             )
+
+    starts = (0, 5, 10, SEAM - 2)
+    for f, (shift_east, shift_west) in enumerate(((-3, -8), (2, -3), (6, 2))):
+        packed = None
+        for h, half in enumerate(halves):
+            large[f][h].wait()
+            for k in half:
+                both = both_edges(fields[f, k, :, 0:LANE], fields[f, k, :, cols - LANE : cols])
+                moved = roll(both, SEAM * k + SUB, 1)
+                packed = moved if packed is None else jnp.where(group == k, moved, packed)
+            if f == 2:
+                for k in half:
+                    pack_rows(k)
+        own_tile[f, inside] = packed
+        seats = (seat >= starts[f]) & (seat < starts[f + 1])
+        to_east[...] = jnp.where(seats, roll(packed, shift_east, 1), spare_east if f == 0 else to_east[...])
+        to_west[...] = jnp.where(seats, roll(packed, shift_west, 1), spare_west if f == 0 else to_west[...])
 
     pl.semaphore_wait(barrier, len(greeted))
 
@@ -230,11 +238,14 @@
             act(item)
 
     start, wait_recv, wait_send = (lambda c: c.start()), (lambda c: c.wait_recv()), (lambda c: c.wait_send())
+    far_east, far_west = my_x == nx - 1, my_x == 0
     pl.when(north_here)(lambda: each(upward[1:], start))
     pl.when(south_here)(lambda: each(downward[1:], start))
-    each(beside, start)
-    pl.when(north_here)(lambda: each(upward[:1], start))
-    pl.when(south_here)(lambda: each(downward[:1], start))
+    pl.when(far_east)(copies[0].start)
+    pl.when(far_west)(copies[1].start)
+    far_up, far_down = my_y == ny // 2 - 1, my_y == ny // 2
+    pl.when(far_up)(upward[0].start)
+    pl.when(far_down)(downward[0].start)
     if rounds:
         tell(0)
 
@@ -251,7 +262,13 @@
         own_sum[...] += jnp.where(col_in[...] > k, thickness[k] * current, 0.0)
         return carry
 
-    lax.fori_loop(0, levels, level, 0, unroll=2)
+    part_way = levels * 1 // 8
+    lax.fori_loop(0, part_way, level, 0, unroll=2)
+    pl.when(north_here & jnp.logical_not(far_up))(upward[0].start)
+    pl.when(south_here & jnp.logical_not(far_down))(downward[0].start)
+    pl.when(jnp.logical_not(far_east))(copies[0].start)
+    pl.when(jnp.logical_not(far_west))(copies[1].start)
+    lax.fori_loop(part_way, levels, level, 0, unroll=2)
 
     def blank(rows_ref, halo):
         rows_ref[...] = jnp.zeros(rows_ref.shape, jnp.float32)
@@ -305,6 +322,8 @@
     depth_lanes = (LANE - SUB + seat) % LANE
     for halo in (low_halo, high_halo):
         own_tile[3, halo] = pick(jnp.where(low_half, flat[0, 0, halo], flat[0, side_block - 1, halo]), depth_lanes)
+    for r in range(0, rows + 2 * SUB, SUB):
+        own_tile[4, at(r)] = roll(own_tile[3, at(r)], -1, 1)
 
     row_sides = ((0, receive_south, 0, SUB, 0, low_halo), (1, receive_north, SUB, 0, rows, high_halo))
     for w, receive, halo_at, own_at, base, halo in row_sides:
@@ -370,28 +389,34 @@
     side_pick = [side_lanes(*bases) for bases in ((2, 0), (6, 6), (10, 10))]
     sides = []
     for got, shifts, first, in_halo in (
-        (west, (3, -2, -6), 3, seat < SUB),
-        (east, (8, 3, -2), 8, seat >= SUB),
+        (west, (3, -2, -6), 3, [seat + d < SUB for d in (0, 1)]),
+        (east, (8, 3, -2), 8, [seat + d >= SUB for d in (0, 1)]),
     ):
-        depth_pick = spare_lane(jnp.minimum(jnp.maximum(seat - first, 0), 4))
-        sides.append((got, shifts, depth_pick, in_halo))
+        depth_picks = [spare_lane(jnp.minimum(jnp.maximum(seat + d - first, 0), 4)) for d in (0, 1)]
+        sides.append((got, shifts, depth_picks, in_halo))
 
     each(beside, wait_recv)
     pl.when(south_here)(lambda: each(upward[1:], wait_recv))
     pl.when(north_here)(lambda: each(downward[1:], wait_recv))
 
-    for r in range(0, rows + 2 * SUB, SUB):
-        for w, (got, shifts, depth_pick, in_halo) in enumerate(sides):
+    tall_rows = range(0, rows + 2 * SUB, SUB)
+    for w, (got, shifts, depth_picks, in_halo) in enumerate(sides):
+        for d, lanes in enumerate(depth_picks):
+            for r in tall_rows:
+                strips[w, 3 + d, at(r)] = jnp.where(in_halo[d], pick(got[at(r)], lanes), own_tile[3 + d, at(r)])
+    for f, lanes in enumerate(side_pick):
+        for r in tall_rows:
+            flat[f, side_block, at(r)] = jnp.where(low_half, pick(east[at(r)], lanes), pick(west[at(r)], lanes))
+    for r in tall_rows:
+        for w, (got, shifts, depth_picks, in_halo) in enumerate(sides):
             sent = got[at(r)]
-            moved = [roll(sent, shift, 1) for shift in shifts] + [pick(sent, depth_pick)]
-            for f in range(4):
-                strips[w, f, at(r)] = jnp.where(in_halo, moved[f], own_tile[f, at(r)])
+            c, e, n = (jnp.where(in_halo[0], roll(sent, shift, 1), own_tile[f, at(r)]) for f, shift in enumerate(shifts))
+            strips[w, 0, at(r)] = c
+            strips[w, 1, at(r)] = jnp.where(jnp.minimum(strips[w, 3, at(r)], strips[w, 4, at(r)]) > strip_level, e, 0.0)
+            strips[w, 2, at(r)] = n
     for r in range(0, rows + 2 * SUB, SUB):
         for w in range(2):
-            deep = strips[w, 3, at(r)]
-            open_east = jnp.minimum(deep, roll(deep, -1, 1)) > strip_level
-            open_nort = jnp.minimum(deep, strips[w, 3, at(r + 1)]) > strip_level
-            strips[w, 1, at(r)] = jnp.where(open_east, strips[w, 1, at(r)], 0.0)
+            open_nort = jnp.minimum(strips[w, 3, at(r)], strips[w, 3, at(r + 1)]) > strip_level
             strips[w, 2, at(r)] = jnp.where(open_nort, strips[w, 2, at(r)], 0.0)
 
     def side_step(w, f, r):
@@ -411,9 +436,6 @@
             new = side_step(w, 4, r)
             strips[w, 5, at(r)] = new
             strips[w, 0, at(r)] = jnp.where(strips[w, 3, at(r)] > strip_level, lane_thickness * new, 0.0)
-    for f, lanes in enumerate(side_pick):
-        for r in range(0, rows + 2 * SUB, SUB):
-            flat[f, side_block, at(r)] = jnp.where(low_half, pick(east[at(r)], lanes), pick(west[at(r)], lanes))
     for r in inner_rows:
         for w in range(2):
             total = strips[w, 0, at(r)]
@@ -569,7 +591,7 @@
         pltpu.VMEM((3, levels, rows, cols), f32),
         pltpu.VMEM((rows, cols), jnp.int32),
         pltpu.VMEM((3, blocks + 1, tall + SUB, LANE), f32),
-        pltpu.VMEM((4, tall, LANE), f32),
+        pltpu.VMEM((5, tall, LANE), f32),
         *[pltpu.VMEM((rows, LANE), f32)] * 2,
         *[pltpu.VMEM((tall, LANE), f32)] * 2,
         *[pltpu.VMEM((levels, blocks, 2 * SUB, LANE), f32)] * 4,
@@ -584,7 +606,7 @@
         pltpu.VMEM((ny * nx - 1, 1, LANE), f32),
         pltpu.SMEM((levels,), f32),
         pltpu.SemaphoreType.REGULAR((max(ny, nx).bit_length(),)),
-        dma((7 + 2 * blocks,)),
+        dma((8 + 2 * blocks,)),
         dma((8,)),
         dma((8,)),
         dma,

time: 20.2 us -> 19.4 us (0.960)
  Pallas kernels: 19.4 us -> 18.6 us
    pallas_call x1, Pallas kernels: 18.3 us -> 17.6 us  [on_device(): pl.pallas_call(functools.partial(kernel, ny, nx), out_shape=(pltpu.VMEM((...]
where the time goes in v4:
time: 19.4 us; the launch traced here: 19.3 us
  Pallas kernels  18.6 us (96%)
  between operations  0.64 us (3%)
    pallas_call x1, Pallas kernels, on_device(): pl.pallas_call(functools.partial(kernel, ny, nx), out_shape=(pltpu.VMEM((...  17.6 us
    pallas_call x1, Pallas kernels, on_device(): pl.pallas_call(finish, out_shape=(jax.ShapeDtypeStruct((levels, rows, col...  1.08 us

profile of v4, /device:TPU:0, one launch (start us, length us, event | category | flops | bytes accessed | tf_op | source)
XLA Modules:
  0.0 19.3 jit_solution(14433732340405636167)
XLA Ops:
  0.6 17.6 %shard_map.86 = (f32[8,128,256]{2,1,0:T(8,128)S(1)}, f32[3,2,128,128]{3,2,1,0:T(8,128)S(1)}, f32[1,128]{1,0:T(1,128)S(1)}) custom-call(f32[8,128,256]{2,1,0:T(8,128)} %tracer_ref.1, f32[8,128,256]{2,1,0:T(8,128)} %east_ref.1, f32[8,128,256]{2,1,0:T(8,128)} %north_ref.1, s32[128,256]{1,0:T(8,128)} %columns_ref.1, f32[8]{0:T(128)} %thick_hbm.1, ...), custom_call_target="tpu_custom_call" | custom-call | tf_op jit(solution)/shard_map/pallas_call | solution.py:615
  18.2 1.1 %shard_map.87 = (f32[8,128,256]{2,1,0:T(8,128)}, f32[128,256]{1,0:T(8,128)}) custom-call(f32[8,128,256]{2,1,0:T(8,128)S(1)} %get-tuple-element.5.tracer_ref, f32[3,2,128,128]{3,2,1,0:T(8,128)S(1)} %get-tuple-element.6.basis_ref, f32[1,128]{1,0:T(1,128)S(1)} %get-tuple-element.7.moments_ref), custom_call_target="tpu_custom_call" | custom-call | tf_op jit(solution)/shard_map/pallas_call | solution.py:627

commit v5 on v4

--- a/solution.py
+++ b/solution.py
@@ -499,7 +499,7 @@
 
     if rounds:
         hear(len(rounds) - 1)
-    for index, target in enumerate(others):
+    for index, target in reversed(list(enumerate(others))):
         pltpu.make_async_remote_copy(
             src_ref=part,
             dst_ref=slots.at[index],
@@ -529,13 +529,12 @@
         device_id=others[0],
         device_id_type=MESH,
     )
-    everything.wait_recv()
-    moments_out[...] = jnp.sum(slots[...], axis=0) + part[...]
-
     everything.wait_send()
     each(beside, wait_send)
     pl.when(north_here)(lambda: each(upward, wait_send))
     pl.when(south_here)(lambda: each(downward, wait_send))
+    everything.wait_recv()
+    moments_out[...] = jnp.sum(slots[...], axis=0) + part[...]
 
 
 def finish(tracer_ref, basis_ref, moments_ref, tracer_out, heights_out, heights, save):

time: 19.4 us -> 19.5 us (level)
  no operation moved by 1% of the time
where the time goes in v5:
time: 19.5 us; the launch traced here: 19.4 us
  Pallas kernels  18.7 us (96%)
  between operations  0.64 us (3%)
    pallas_call x1, Pallas kernels, on_device(): pl.pallas_call(functools.partial(kernel, ny, nx), out_shape=(pltpu.VMEM((...  17.6 us
    pallas_call x1, Pallas kernels, on_device(): pl.pallas_call(finish, out_shape=(jax.ShapeDtypeStruct((levels, rows, col...  1.08 us

profile of v5, /device:TPU:0, one launch (start us, length us, event | category | flops | bytes accessed | tf_op | source)
XLA Modules:
  0.0 19.4 jit_solution(458019074430335884)
XLA Ops:
  0.6 17.6 %shard_map.86 = (f32[8,128,256]{2,1,0:T(8,128)S(1)}, f32[3,2,128,128]{3,2,1,0:T(8,128)S(1)}, f32[1,128]{1,0:T(1,128)S(1)}) custom-call(f32[8,128,256]{2,1,0:T(8,128)} %tracer_ref.1, f32[8,128,256]{2,1,0:T(8,128)} %east_ref.1, f32[8,128,256]{2,1,0:T(8,128)} %north_ref.1, s32[128,256]{1,0:T(8,128)} %columns_ref.1, f32[8]{0:T(128)} %thick_hbm.1, ...), custom_call_target="tpu_custom_call" | custom-call | tf_op jit(solution)/shard_map/pallas_call | solution.py:614
  18.3 1.1 %shard_map.87 = (f32[8,128,256]{2,1,0:T(8,128)}, f32[128,256]{1,0:T(8,128)}) custom-call(f32[8,128,256]{2,1,0:T(8,128)S(1)} %get-tuple-element.5.tracer_ref, f32[3,2,128,128]{3,2,1,0:T(8,128)S(1)} %get-tuple-element.6.basis_ref, f32[1,128]{1,0:T(1,128)S(1)} %get-tuple-element.7.moments_ref), custom_call_target="tpu_custom_call" | custom-call | tf_op jit(solution)/shard_map/pallas_call | solution.py:626

commit v6 on v5

--- a/solution.py
+++ b/solution.py
@@ -396,24 +396,27 @@
         sides.append((got, shifts, depth_picks, in_halo))
 
     each(beside, wait_recv)
+
+    def unpack(tall_rows):
+        for w, (got, shifts, depth_picks, in_halo) in enumerate(sides):
+            for d, lanes in enumerate(depth_picks):
+                for r in tall_rows:
+                    strips[w, 3 + d, at(r)] = jnp.where(in_halo[d], pick(got[at(r)], lanes), own_tile[3 + d, at(r)])
+        for f, lanes in enumerate(side_pick):
+            for r in tall_rows:
+                flat[f, side_block, at(r)] = jnp.where(low_half, pick(east[at(r)], lanes), pick(west[at(r)], lanes))
+        for r in tall_rows:
+            for w, (got, shifts, depth_picks, in_halo) in enumerate(sides):
+                sent = got[at(r)]
+                c, e, n = (jnp.where(in_halo[0], roll(sent, shift, 1), own_tile[f, at(r)]) for f, shift in enumerate(shifts))
+                strips[w, 0, at(r)] = c
+                strips[w, 1, at(r)] = jnp.where(jnp.minimum(strips[w, 3, at(r)], strips[w, 4, at(r)]) > strip_level, e, 0.0)
+                strips[w, 2, at(r)] = n
+
+    unpack(range(SUB, rows + SUB, SUB))
     pl.when(south_here)(lambda: each(upward[1:], wait_recv))
     pl.when(north_here)(lambda: each(downward[1:], wait_recv))
-
-    tall_rows = range(0, rows + 2 * SUB, SUB)
-    for w, (got, shifts, depth_picks, in_halo) in enumerate(sides):
-        for d, lanes in enumerate(depth_picks):
-            for r in tall_rows:
-                strips[w, 3 + d, at(r)] = jnp.where(in_halo[d], pick(got[at(r)], lanes), own_tile[3 + d, at(r)])
-    for f, lanes in enumerate(side_pick):
-        for r in tall_rows:
-            flat[f, side_block, at(r)] = jnp.where(low_half, pick(east[at(r)], lanes), pick(west[at(r)], lanes))
-    for r in tall_rows:
-        for w, (got, shifts, depth_picks, in_halo) in enumerate(sides):
-            sent = got[at(r)]
-            c, e, n = (jnp.where(in_halo[0], roll(sent, shift, 1), own_tile[f, at(r)]) for f, shift in enumerate(shifts))
-            strips[w, 0, at(r)] = c
-            strips[w, 1, at(r)] = jnp.where(jnp.minimum(strips[w, 3, at(r)], strips[w, 4, at(r)]) > strip_level, e, 0.0)
-            strips[w, 2, at(r)] = n
+    unpack((0, rows + SUB))
     for r in range(0, rows + 2 * SUB, SUB):
         for w in range(2):
             open_nort = jnp.minimum(strips[w, 3, at(r)], strips[w, 3, at(r + 1)]) > strip_level

time: 19.5 us -> 19.6 us (level)
  no operation moved by 1% of the time
where the time goes in v6:
time: 19.6 us; the launch traced here: 19.4 us
  Pallas kernels  18.8 us (96%)
  between operations  0.64 us (3%)
    pallas_call x1, Pallas kernels, on_device(): pl.pallas_call(functools.partial(kernel, ny, nx), out_shape=(pltpu.VMEM((...  17.7 us
    pallas_call x1, Pallas kernels, on_device(): pl.pallas_call(finish, out_shape=(jax.ShapeDtypeStruct((levels, rows, col...  1.08 us

profile of v6, /device:TPU:0, one launch (start us, length us, event | category | flops | bytes accessed | tf_op | source)
XLA Modules:
  0.0 19.4 jit_solution(1249687423010147954)
XLA Ops:
  0.6 17.7 %shard_map.86 = (f32[8,128,256]{2,1,0:T(8,128)S(1)}, f32[3,2,128,128]{3,2,1,0:T(8,128)S(1)}, f32[1,128]{1,0:T(1,128)S(1)}) custom-call(f32[8,128,256]{2,1,0:T(8,128)} %tracer_ref.1, f32[8,128,256]{2,1,0:T(8,128)} %east_ref.1, f32[8,128,256]{2,1,0:T(8,128)} %north_ref.1, s32[128,256]{1,0:T(8,128)} %columns_ref.1, f32[8]{0:T(128)} %thick_hbm.1, ...), custom_call_target="tpu_custom_call" | custom-call | tf_op jit(solution)/shard_map/pallas_call | solution.py:617
  18.4 1.1 %shard_map.87 = (f32[8,128,256]{2,1,0:T(8,128)}, f32[128,256]{1,0:T(8,128)}) custom-call(f32[8,128,256]{2,1,0:T(8,128)S(1)} %get-tuple-element.5.tracer_ref, f32[3,2,128,128]{3,2,1,0:T(8,128)S(1)} %get-tuple-element.6.basis_ref, f32[1,128]{1,0:T(1,128)S(1)} %get-tuple-element.7.moments_ref), custom_call_target="tpu_custom_call" | custom-call | tf_op jit(solution)/shard_map/pallas_call | solution.py:629
